TPU v7x, 32 devices: a whole 2x2x4 slice. The times are simulated.
32 devices in a mesh: gy: 16 (over z, y, core), gz: 2 (over x).
Axes of the slice: x: 2, y: 2, z: 4, core: 2. Of those that a mesh axis runs over, the one named last changes fastest.
Arguments:
- random_fields: bfloat16 [16, 3, 2048, 512], P(None, None, 'gy', 'gz'), may hold values from -6 to 6
- previous: float32 [3, 2048, 512], P(None, 'gy', 'gz'), may hold values from -6 to 6
- decay: float32 [3, 512], P(None, 'gz'), may hold values from 0.2 to 0.95
- mean_flow: float32 [3, 512], P(None, 'gz'), may hold values from 0 to 1.5
- lund_diag: float32 [3, 512], P(None, 'gz'), may hold values from 0.3 to 1.5
- lund_off: float32 [3, 512], P(None, 'gz'), may hold values from -0.6 to 0.6
Outputs:
- velocity: float32 [16, 3, 2048, 512], P(None, None, 'gy', 'gz')
All inputs are finite; a program needn't handle non-finite values.
Results may differ from a plain program's by a relative error of at most 0.0015.
The roundings to bfloat16 on the way count: a program that leaves them out, or rounds other values in their place, can miss the bound.
Values may be sent and summed in bfloat16 or wider, within the bound.
No kernel may reach another device: no remote copies, remote signals or barrier semaphores. Data moves between devices by JAX's collectives and lax.ppermute only.
A program may use at most 128 MiB of HBM per device.

v0:
```python
import functools
import math

import jax
import jax.numpy as jnp
from jax import lax
from jax.experimental import pallas as pl
from jax.experimental.pallas import tpu as pltpu
from jax.sharding import PartitionSpec as P

HALF = 96


def taps(lag):
    offsets = jnp.arange(-HALF, HALF + 1).astype(jnp.float32)
    scale = HALF * 1.0
    kernel = jnp.exp(-math.pi * offsets * offsets / (2.0 * scale * scale))
    norm = jnp.sqrt(jnp.sum(kernel * kernel))
    lag = lag.astype(jnp.float32)
    value = jnp.exp(-math.pi * lag * lag / (2.0 * scale * scale)) / norm
    return jnp.where(jnp.abs(lag) <= HALF, value, jnp.zeros_like(value)).astype(jnp.bfloat16)


def pairs(count, first, closed):
    found = []
    for low in range(first, count, 2):
        if low + 1 < count or closed:
            high = (low + 1) % count
            found += [(low, high), (high, low)]
    return found


def span_product(weights, core, own, link):
    planes = [jnp.concatenate([core[p], own[p], link[p]], axis=0) for p in range(len(own))]
    return jnp.dot(weights, jnp.concatenate(planes, axis=1), preferred_element_type=jnp.float32)


def smooth_far(block, start, first, count, where, weights, own, core, link):
    parts, lanes = own.shape[1], core.shape[3]
    lane = pl.multiple_of(where[block] * lanes, lanes)
    index = [(t, c) for t in range(count) for c in range(parts)]
    product = span_product(
        weights[...],
        [core[start + first + t, c] for t, c in index],
        [own[start + first + t, c, :, pl.ds(lane, lanes)] for t, c in index],
        [link[first + t, c] for t, c in index],
    ).astype(own.dtype)
    return {i: product[:, p * lanes : (p + 1) * lanes] for p, i in enumerate(index)}


def smooth_kernel(start, block, per, where, weights, own, core, link, out, edge):
    steps = out.shape[0]
    width = edge.shape[2]
    for first in range(0, steps, per):
        planes = smooth_far(block, start, first, min(per, steps - first), where, weights, own, core, link)
        for (t, c), plane in planes.items():
            out[first + t, c] = plane
            turned = plane.T

            @pl.when(where[block] == 1)
            def _():
                edge[first + t, c] = turned[turned.shape[0] - width :, :]

            @pl.when(where[block] == 0)
            def _():
                edge[first + t, c] = turned[:width, :]


def velocity_kernel(halos, raw, start, near_first, per, where, weights, walls, *refs):
    (decay, mean, diag, off, before, own, core, link, near), rest = refs[:9], refs[9:]
    beside = rest[:halos]
    velocity, state = rest[-2:]
    parts, rows = own.shape[1:3]

    @pl.when(pl.program_id(0) == 0)
    def _():
        state[...] = before[...]

    first = pl.program_id(0) * per
    if raw:
        far = smooth_far(1, start, first, per, where, weights, own, core, link)
    else:
        far = {(t, c): own[first + t, c] for t in range(per) for c in range(parts)}
    index = [(t, c) for t in range(per) for c in range(parts)]
    cells = []
    for t, c in index:
        at = near_first + first + t
        cells.append(jnp.concatenate([far[t, c], near[at, c]] + [halo(first + t, c) for halo in halo_readers(beside, near_first)], axis=1))
    filtered = jnp.dot(jnp.concatenate(cells, axis=0), walls[...], preferred_element_type=jnp.float32)
    keep = decay[...]
    fresh = jnp.sqrt(1.0 - keep * keep)
    line = lambda x, c: x[c : c + 1, :]
    u, d, o = mean[...], diag[...], off[...]
    now = [state[c] for c in range(parts)]
    for t in range(per):
        for c in range(parts):
            p = t * parts + c
            now[c] = line(keep, c) * now[c] + line(fresh, c) * filtered[p * rows : (p + 1) * rows]
        velocity[t, 0] = line(u, 0) + line(d, 0) * now[0]
        velocity[t, 1] = line(u, 1) + line(o, 0) * now[0] + line(d, 1) * now[1]
        velocity[t, 2] = line(u, 2) + line(o, 1) * now[0] + line(o, 2) * now[1] + line(d, 2) * now[2]
    for c in range(parts):
        state[c] = now[c]


def halo_readers(beside, near_first):
    offsets = [near_first, 0]
    return [lambda t, c, ref=ref, o=o: ref[o + t, c].T for ref, o in zip(beside, offsets)]


def chunks_of(steps):
    half, last = steps // 2, max(1, steps // 4)
    return [(0, half), (half, steps - half)], [(0, half), (half, steps - half - last), (steps - last, last)]


def shards(random_fields, previous, decay, mean_flow, lund_diag, lund_off):
    steps, parts, rows, cols = random_fields.shape
    lanes = cols // 2
    span_count = lax.axis_size("gy")
    wall_count = lax.axis_size("gz")
    odd = lax.axis_index("gy") % 2
    wall_odd = lax.axis_index("gz") % 2
    near_block = 1 - wall_odd
    far_block = wall_odd
    where = jnp.stack([near_block, far_block]).astype(jnp.int32)

    core_pairs = pairs(span_count, 0, True)
    link_pairs = pairs(span_count, 1, True)
    near_pairs = pairs(wall_count, 0, False)
    far_pairs = pairs(wall_count, 1, False)

    near_chunks, far_chunks = chunks_of(steps)
    whole = pl.BlockSpec(memory_space=pltpu.VMEM)

    link_row, core_row = odd * (rows - HALF), (1 - odd) * (rows - HALF)

    def cut(fields, start, count, row, block):
        return lax.dynamic_slice(fields, (start, 0, row, block * lanes), (count, parts, HALF, lanes))

    first_cut = cut(random_fields, *near_chunks[0], link_row, near_block)
    fields, first_cut = lax.optimization_barrier((random_fields, first_cut))
    near_cuts = [first_cut] + [cut(fields, s, n, link_row, near_block) for s, n in near_chunks[1:]]
    far_cuts = [cut(fields, s, n, link_row, far_block) for s, n in far_chunks]
    near_core = lax.ppermute(cut(fields, 0, steps, core_row, near_block), "gy", core_pairs)
    far_core = lax.ppermute(cut(fields, 0, steps, core_row, far_block), "gy", core_pairs)
    links = [lax.ppermute(x, "gy", link_pairs) for x in near_cuts + far_cuts]
    near_link, far_link = links[: len(near_chunks)], links[len(near_chunks) :]

    i = jnp.arange(rows)[:, None]
    j = jnp.arange(HALF)[None, :]
    left, right = j - HALF - i, rows + j - i
    weights = taps(
        jnp.concatenate(
            [jnp.where(odd == 1, left, right), jnp.arange(rows)[None, :] - i, jnp.where(odd == 1, right, left)], axis=1
        )
    )
    m = jnp.arange(cols)[None, :]
    j = jnp.arange(lanes)[:, None]
    h = jnp.arange(HALF)[:, None]
    before_block, after_block = h - HALF - m, cols + h - m
    columns = [far_block * lanes + j - m, near_block * lanes + j - m]
    if near_pairs:
        columns.append(jnp.where(wall_odd == 1, before_block, after_block))
    if far_pairs:
        columns.append(jnp.where(wall_odd == 1, after_block, before_block))
    walls = taps(jnp.concatenate(columns, axis=0))
    weights, walls = lax.optimization_barrier((weights, walls))

    def smooth(start, count, block, core, link):
        return pl.pallas_call(
            functools.partial(smooth_kernel, start, block, 4),
            out_shape=(
                jax.ShapeDtypeStruct((count, parts, rows, lanes), jnp.bfloat16),
                jax.ShapeDtypeStruct((count, parts, HALF, rows), jnp.bfloat16),
            ),
            in_specs=[pl.BlockSpec(memory_space=pltpu.SMEM)] + [whole] * 4,
            out_specs=(whole, whole),
            compiler_params=pltpu.CompilerParams(vmem_limit_bytes=12 * 2**20),
            cost_estimate=pl.CostEstimate(
                flops=2 * count * parts * rows * lanes * (rows + 2 * HALF),
                bytes_accessed=4 * count * parts * lanes * (rows + HALF),
                transcendentals=0,
            ),
            name="smooth",
        )(where, weights, random_fields, core, link)

    near = [smooth(s, n, 0, near_core, link) for (s, n), link in zip(near_chunks, near_link)]
    near_halo = []
    if near_pairs:
        near_halo = [lax.ppermute(edge, "gz", near_pairs) for _, edge in near]
    far, far_halo = None, []
    if far_pairs:
        far = [smooth(s, n, 1, far_core, link) for (s, n), link in zip(far_chunks, far_link)]
        far_halo = [lax.ppermute(edge, "gz", far_pairs) for _, edge in far]

    velocity, state = None, previous
    for k, (s, n) in enumerate(far_chunks):
        source = max(q for q, (start, _) in enumerate(near_chunks) if start <= s)
        per = math.gcd(math.gcd(n, s), 2)
        operands = [where, weights, walls, decay, mean_flow, lund_diag, lund_off, state]
        operands += [random_fields if far is None else far[k][0], far_core, far_link[k], near[source][0]]
        beside = near_halo[source : source + 1] + far_halo[k : k + 1]
        operands += beside
        specs = [pl.BlockSpec(memory_space=pltpu.SMEM)] + [whole] * (len(operands) - 1)
        aliases = {}
        if velocity is not None:
            aliases = {len(operands): 0}
            operands.append(velocity)
            specs.append(pl.BlockSpec(memory_space=pl.ANY))
        velocity, state = pl.pallas_call(
            functools.partial(
                velocity_kernel, len(beside), far is None, s, s - near_chunks[source][0], per
            ),
            out_shape=(
                jax.ShapeDtypeStruct((steps, parts, rows, cols), jnp.float32),
                jax.ShapeDtypeStruct(previous.shape, jnp.float32),
            ),
            grid=(n // per,),
            in_specs=specs,
            out_specs=(
                pl.BlockSpec((per, parts, rows, cols), functools.partial(lambda o, t: (o + t, 0, 0, 0), s // per)),
                whole,
            ),
            input_output_aliases=aliases,
            compiler_params=pltpu.CompilerParams(vmem_limit_bytes=12 * 2**20),
            cost_estimate=pl.CostEstimate(
                flops=2 * n * parts * rows * (lanes * (rows + 2 * HALF) + cols * walls.shape[0]),
                bytes_accessed=n * parts * rows * (4 * cols + 10 * lanes),
                transcendentals=0,
            ),
            name="velocity",
        )(*operands)
    return velocity


def solution(mesh):
    return jax.shard_map(
        shards,
        mesh=mesh,
        in_specs=(
            P(None, None, "gy", "gz"),
            P(None, "gy", "gz"),
            P(None, "gz"),
            P(None, "gz"),
            P(None, "gz"),
            P(None, "gz"),
        ),
        out_specs=P(None, None, "gy", "gz"),
        check_vma=False,
    )
```

profile of v0, /device:TPU:1, one launch (start us, length us, event | category | flops | bytes accessed | tf_op | source)
XLA Modules:
  0.0 64.8 jit_solution(5276528430712260492)
XLA Ops:
  0.0 0.0 copy-start
  0.0 2.1 %constant_dynamic-slice_fusion.6 = bf16[8,3,96,128]{3,2,1,0:T(8,128)(2,1)} fusion(bf16[16,3,128,256]{3,2,1,0:T(8,128)(2,1)} %refs_5_.5, s32[]{:T(128)S(6)} %select_n.70, s32[]{:T(128)S(6)} %select_n.71), kind=kLoop, calls=%fused_computation.30 | loop fusion | bytes 1179656 | tf_op jit(solution)/shard_map/dynamic_slice | solution.py:138
  2.1 2.6 %collective-permute-start.3 = (bf16[8,3,96,128]{3,2,1,0:T(8,128)(2,1)}, bf16[8,3,96,128]{3,2,1,0:T(8,128)(2,1)}, u32[]{:S(2)}, u32[]{:S(2)}) collective-permute-start(bf16[8,3,96,128]{3,2,1,0:T(8,128)(2,1)} %constant_dynamic-slice_fusion.6), channel_id=1, source_target_pairs={{2,4},{4,2},{6,8},{8,6},{10,12},{12,10},{14,16},{16,14},{18,20},{2... | collective-permute-start | bytes 1769480 | tf_op jit(solution)/shard_map/ppermute | solution.py:146
  4.7 2.4 %constant_dynamic-slice_fusion.1 = (bf16[8,3,96,128]{3,2,1,0:T(8,128)(2,1)}, bf16[8,3,96,128]{3,2,1,0:T(8,128)(2,1)}) fusion(bf16[16,3,128,256]{3,2,1,0:T(8,128)(2,1)} %refs_5_.5, s32[]{:T(128)S(6)} %select_n.70, s32[]{:T(128)S(6)} %select_n.71, s32[]{:T(128)S(6)} %select_n.73), kind=kLoop, calls=%fused_computation.25 | loop fusion | bytes 2359308 | tf_op jit(solution)/shard_map/dynamic_slice | solution.py:138
  7.1 0.0 collective-permute-start.6
  7.1 1.7 %collective-permute-start.1 = (bf16[8,3,96,128]{3,2,1,0:T(8,128)(2,1)}, bf16[8,3,96,128]{3,2,1,0:T(8,128)(2,1)}, u32[]{:S(2)}, u32[]{:S(2)}) collective-permute-start(bf16[8,3,96,128]{3,2,1,0:T(8,128)(2,1)} %get-tuple-element.34), channel_id=1, source_target_pairs={{2,4},{4,2},{6,8},{8,6},{10,12},{12,10},{14,16},{16,14},{18,20},{2... | collective-permute-start | bytes 1769480 | tf_op jit(solution)/shard_map/ppermute | solution.py:146
  8.8 0.0 copy-done
  8.8 1.8 %constant_dynamic-slice_fusion.3 = (bf16[16,3,96,128]{3,2,1,0:T(8,128)(2,1)}, bf16[16,3,96,128]{3,2,1,0:T(8,128)(2,1)}) fusion(bf16[16,3,128,256]{3,2,1,0:T(8,128)(2,1)S(1)} %copy-done, s32[]{:T(128)S(6)} %select_n.72, s32[]{:T(128)S(6)} %select_n.71, s32[]{:T(128)S(6)} %select_n.73), kind=kLoop, calls=%fused_computation.27 | loop fusion | bytes 4718604 | tf_op jit(solution)/shard_map/dynamic_slice | solution.py:138
  10.7 5.6 %collective-permute-start.2 = (bf16[16,3,96,128]{3,2,1,0:T(8,128)(2,1)}, bf16[16,3,96,128]{3,2,1,0:T(8,128)(2,1)}, u32[]{:S(2)}, u32[]{:S(2)}) collective-permute-start(bf16[16,3,96,128]{3,2,1,0:T(8,128)(2,1)} %get-tuple-element.35), channel_id=1, source_target_pairs={{0,2},{2,0},{4,6},{6,4},{8,10},{10,8},{12,14},{14,12},{16,18},{18,... | collective-permute-start | bytes 3538952 | tf_op jit(solution)/shard_map/ppermute | solution.py:144
  16.2 0.0 collective-permute-start
  16.2 0.1 subtract_select_fusion
  16.4 0.6 fusion.15
  17.6 0.1 iota_subtract_fusion.1
  17.7 0.1 iota_subtract_fusion
  17.7 0.1 fusion.4.walls
  17.9 0.2 fusion.9.weights
  18.1 0.1 pad_add_fusion.where
  18.2 19.0 %collective-permute-done.3.link = bf16[8,3,96,128]{3,2,1,0:T(8,128)(2,1)} collective-permute-done((bf16[8,3,96,128]{3,2,1,0:T(8,128)(2,1)}, bf16[8,3,96,128]{3,2,1,0:T(8,128)(2,1)}, u32[]{:S(2)}, u32[]{:S(2)}) %collective-permute-start.3) | collective-permute-done | bytes 589856 | tf_op jit(solution)/shard_map/ppermute | solution.py:146
  37.1 0.0 collective-permute-done.2.core
  37.1 3.7 %smooth.2 = (bf16[8,3,128,128]{3,2,1,0:T(8,128)(2,1)S(1)}, bf16[8,3,96,128]{3,2,1,0:T(8,128)(2,1)S(1)}) custom-call(s32[2]{0:T(128)S(1)} %pad_add_fusion.where, bf16[128,320]{1,0:T(8,128)(2,1)S(1)} %fusion.9.weights, bf16[16,3,128,256]{3,2,1,0:T(8,128)(2,1)S(1)} %copy-done, bf16[16,3,96,128]{3,2,1,0:T(8,128)(2,1)} %collective-permute-done.2.core, ...), custom_call_target="tpu_custom_call" | custom-call | flops 251658240 | bytes 2752512 | tf_op jit(solution)/shard_map/smooth/pallas_call | solution.py:170
  40.9 0.0 copy-start.1
  40.9 0.0 copy-start.2
  40.9 0.0 copy-start.3
  40.9 0.0 copy-start.4
  40.9 0.0 copy-start.5
  40.9 1.3 %collective-permute-start.4 = (bf16[8,3,96,128]{3,2,1,0:T(8,128)(2,1)S(1)}, bf16[8,3,96,128]{3,2,1,0:T(8,128)(2,1)S(1)}, u32[]{:S(2)}, u32[]{:S(2)}) collective-permute-start(bf16[8,3,96,128]{3,2,1,0:T(8,128)(2,1)S(1)} %get-tuple-element.23), channel_id=1, source_target_pairs={{0,1},{1,0},{2,3},{3,2},{4,5},{5,4},{6,7},{7,6},{8,9},{9,8},{10,11... | collective-permute-start | bytes 1769480 | tf_op jit(solution)/shard_map/ppermute | solution.py:190
  42.2 1.9 %collective-permute-done.6.link = bf16[8,3,96,128]{3,2,1,0:T(8,128)(2,1)} collective-permute-done((bf16[8,3,96,128]{3,2,1,0:T(8,128)(2,1)}, bf16[8,3,96,128]{3,2,1,0:T(8,128)(2,1)}, u32[]{:S(2)}, u32[]{:S(2)}) %collective-permute-start.6) | collective-permute-done | bytes 589856 | tf_op jit(solution)/shard_map/ppermute | solution.py:146
  44.2 3.7 %smooth.3 = (bf16[8,3,128,128]{3,2,1,0:T(8,128)(2,1)S(1)}, bf16[8,3,96,128]{3,2,1,0:T(8,128)(2,1)S(1)}) custom-call(s32[2]{0:T(128)S(1)} %pad_add_fusion.where, bf16[128,320]{1,0:T(8,128)(2,1)S(1)} %fusion.9.weights, bf16[16,3,128,256]{3,2,1,0:T(8,128)(2,1)S(1)} %copy-done, bf16[16,3,96,128]{3,2,1,0:T(8,128)(2,1)} %collective-permute-done.2.core, ...), custom_call_target="tpu_custom_call" | custom-call | flops 251658240 | bytes 2752512 | tf_op jit(solution)/shard_map/smooth/pallas_call | solution.py:170
  47.9 1.3 %collective-permute-start.7 = (bf16[8,3,96,128]{3,2,1,0:T(8,128)(2,1)S(1)}, bf16[8,3,96,128]{3,2,1,0:T(8,128)(2,1)S(1)}, u32[]{:S(2)}, u32[]{:S(2)}) collective-permute-start(bf16[8,3,96,128]{3,2,1,0:T(8,128)(2,1)S(1)} %get-tuple-element.26), channel_id=1, source_target_pairs={{0,1},{1,0},{2,3},{3,2},{4,5},{5,4},{6,7},{7,6},{8,9},{9,8},{10,11... | collective-permute-start | bytes 1769480 | tf_op jit(solution)/shard_map/ppermute | solution.py:190
  49.2 0.1 constant_dynamic-slice_fusion
  49.3 2.1 %collective-permute-start.5 = (bf16[4,3,96,128]{3,2,1,0:T(8,128)(2,1)S(1)}, bf16[4,3,96,128]{3,2,1,0:T(8,128)(2,1)S(1)}, u32[]{:S(2)}, u32[]{:S(2)}) collective-permute-start(bf16[4,3,96,128]{3,2,1,0:T(8,128)(2,1)S(1)} %get-tuple-element.32), channel_id=1, source_target_pairs={{2,4},{4,2},{6,8},{8,6},{10,12},{12,10},{14,16},{16,14},{18,20},{2... | collective-permute-start | bytes 884744 | tf_op jit(solution)/shard_map/ppermute | solution.py:146
  51.4 0.0 collective-permute-done.1.refs_7_
  51.4 0.8 %collective-permute-start.8 = (bf16[4,3,96,128]{3,2,1,0:T(8,128)(2,1)S(1)}, bf16[4,3,96,128]{3,2,1,0:T(8,128)(2,1)S(1)}, u32[]{:S(2)}, u32[]{:S(2)}) collective-permute-start(bf16[4,3,96,128]{3,2,1,0:T(8,128)(2,1)S(1)} %get-tuple-element.31), channel_id=1, source_target_pairs={{2,4},{4,2},{6,8},{8,6},{10,12},{12,10},{14,16},{16,14},{18,20},{2... | collective-permute-start | bytes 884744 | tf_op jit(solution)/shard_map/ppermute | solution.py:146
  52.2 0.0 collective-permute-done.refs_6_
  52.2 0.0 collective-permute-done.4.refs_9_
  52.3 0.0 copy-done.1
  52.3 0.0 copy-done.2
  52.3 0.0 copy-done.3
  52.3 0.0 copy-done.4
  52.3 0.0 copy-done.5
  52.3 5.3 %velocity.3 = (f32[16,3,128,256]{3,2,1,0:T(8,128)}, f32[3,128,256]{2,1,0:T(8,128)S(1)}) custom-call(s32[2]{0:T(128)S(1)} %pad_add_fusion.where, bf16[128,320]{1,0:T(8,128)(2,1)S(1)} %fusion.9.weights, bf16[352,256]{1,0:T(8,128)(2,1)S(1)} %fusion.4.walls, f32[3,256]{1,0:T(4,128)S(1)} %copy-done.2, f32[3,256]{1,0:T(4,128)S(1)} %copy-done.3, ...), custom_call_target="tpu_custom_call" | custom-call | flops 805306368 | bytes 7077888 | tf_op jit(solution)/shard_map/velocity/pallas_call | solution.py:210
  57.6 0.0 collective-permute-done.5.refs_7_
  57.6 0.0 collective-permute-done.7.refs_9_
  57.6 3.6 %velocity.4 = (f32[16,3,128,256]{3,2,1,0:T(8,128)}, f32[3,128,256]{2,1,0:T(8,128)S(1)}) custom-call(s32[2]{0:T(128)S(1)} %pad_add_fusion.where, bf16[128,320]{1,0:T(8,128)(2,1)S(1)} %fusion.9.weights, bf16[352,256]{1,0:T(8,128)(2,1)S(1)} %fusion.4.walls, f32[3,256]{1,0:T(4,128)S(1)} %copy-done.2, ...), custom_call_target="tpu_custom_call", output_to_operand_aliasing={{0}: (13, {})} | custom-call | flops 402653184 | bytes 3538944 | tf_op jit(solution)/shard_map/velocity/pallas_call | solution.py:210
  61.2 0.0 collective-permute-done.8.refs_7_
  61.2 3.7 %velocity.5 = (f32[16,3,128,256]{3,2,1,0:T(8,128)}, f32[3,128,256]{2,1,0:T(8,128)}) custom-call(s32[2]{0:T(128)S(1)} %pad_add_fusion.where, bf16[128,320]{1,0:T(8,128)(2,1)S(1)} %fusion.9.weights, bf16[352,256]{1,0:T(8,128)(2,1)S(1)} %fusion.4.walls, f32[3,256]{1,0:T(4,128)S(1)} %copy-done.2, ...), custom_call_target="tpu_custom_call", output_to_operand_aliasing={{0}: (13, {})} | custom-call | flops 402653184 | bytes 3538944 | tf_op jit(solution)/shard_map/velocity/pallas_call | solution.py:210
  (6 shorter events, 0.0 us)
Async XLA Ops:
  0.0 8.8 %copy-start = (bf16[16,3,128,256]{3,2,1,0:T(8,128)(2,1)S(1)}, bf16[16,3,128,256]{3,2,1,0:T(8,128)(2,1)}, u32[]{:S(2)}) copy-start(bf16[16,3,128,256]{3,2,1,0:T(8,128)(2,1)} %refs_5_.5) | copy-start | bytes 9437188
  2.1 35.0 %collective-permute-start.3 = (bf16[8,3,96,128]{3,2,1,0:T(8,128)(2,1)}, bf16[8,3,96,128]{3,2,1,0:T(8,128)(2,1)}, u32[]{:S(2)}, u32[]{:S(2)}) collective-permute-start(bf16[8,3,96,128]{3,2,1,0:T(8,128)(2,1)} %constant_dynamic-slice_fusion.6), channel_id=1, source_target_pairs={{2,4},{4,2},{6,8},{8,6},{10,12},{12,10},{14,16},{16,14},{18,20},{2... | collective-permute-start | bytes 1769480 | tf_op jit(solution)/shard_map/ppermute | solution.py:146
  7.1 37.1 %collective-permute-start.6 = (bf16[8,3,96,128]{3,2,1,0:T(8,128)(2,1)}, bf16[8,3,96,128]{3,2,1,0:T(8,128)(2,1)}, u32[]{:S(2)}, u32[]{:S(2)}) collective-permute-start(bf16[8,3,96,128]{3,2,1,0:T(8,128)(2,1)} %get-tuple-element.33), channel_id=1, source_target_pairs={{2,4},{4,2},{6,8},{8,6},{10,12},{12,10},{14,16},{16,14},{18,20},{2... | collective-permute-start | bytes 1769480 | tf_op jit(solution)/shard_map/ppermute | solution.py:146
  7.1 44.4 %collective-permute-start.1 = (bf16[8,3,96,128]{3,2,1,0:T(8,128)(2,1)}, bf16[8,3,96,128]{3,2,1,0:T(8,128)(2,1)}, u32[]{:S(2)}, u32[]{:S(2)}) collective-permute-start(bf16[8,3,96,128]{3,2,1,0:T(8,128)(2,1)} %get-tuple-element.34), channel_id=1, source_target_pairs={{2,4},{4,2},{6,8},{8,6},{10,12},{12,10},{14,16},{16,14},{18,20},{2... | collective-permute-start | bytes 1769480 | tf_op jit(solution)/shard_map/ppermute | solution.py:146
  10.7 26.5 %collective-permute-start.2 = (bf16[16,3,96,128]{3,2,1,0:T(8,128)(2,1)}, bf16[16,3,96,128]{3,2,1,0:T(8,128)(2,1)}, u32[]{:S(2)}, u32[]{:S(2)}) collective-permute-start(bf16[16,3,96,128]{3,2,1,0:T(8,128)(2,1)} %get-tuple-element.35), channel_id=1, source_target_pairs={{0,2},{2,0},{4,6},{6,4},{8,10},{10,8},{12,14},{14,12},{16,18},{18,... | collective-permute-start | bytes 3538952 | tf_op jit(solution)/shard_map/ppermute | solution.py:144
  16.2 36.0 %collective-permute-start = (bf16[16,3,96,128]{3,2,1,0:T(8,128)(2,1)}, bf16[16,3,96,128]{3,2,1,0:T(8,128)(2,1)}, u32[]{:S(2)}, u32[]{:S(2)}) collective-permute-start(bf16[16,3,96,128]{3,2,1,0:T(8,128)(2,1)} %get-tuple-element.36), channel_id=1, source_target_pairs={{0,2},{2,0},{4,6},{6,4},{8,10},{10,8},{12,14},{14,12},{16,18},{18,... | collective-permute-start | bytes 3538952 | tf_op jit(solution)/shard_map/ppermute | solution.py:145
  40.9 11.4 %copy-start.1 = (f32[3,128,256]{2,1,0:T(8,128)S(1)}, f32[3,128,256]{2,1,0:T(8,128)}, u32[]{:S(2)}) copy-start(f32[3,128,256]{2,1,0:T(8,128)} %refs_4_.1) | copy-start | bytes 1179652
  40.9 11.4 %copy-start.2 = (f32[3,256]{1,0:T(4,128)S(1)}, f32[3,256]{1,0:T(4,128)}, u32[]{:S(2)}) copy-start(f32[3,256]{1,0:T(4,128)} %refs_0_.5) | copy-start | bytes 9220
  40.9 11.4 %copy-start.3 = (f32[3,256]{1,0:T(4,128)S(1)}, f32[3,256]{1,0:T(4,128)}, u32[]{:S(2)}) copy-start(f32[3,256]{1,0:T(4,128)} %refs_1_.5) | copy-start | bytes 9220
  40.9 11.4 %copy-start.4 = (f32[3,256]{1,0:T(4,128)S(1)}, f32[3,256]{1,0:T(4,128)}, u32[]{:S(2)}) copy-start(f32[3,256]{1,0:T(4,128)} %refs_2_.5) | copy-start | bytes 9220
  40.9 11.4 %copy-start.5 = (f32[3,256]{1,0:T(4,128)S(1)}, f32[3,256]{1,0:T(4,128)}, u32[]{:S(2)}) copy-start(f32[3,256]{1,0:T(4,128)} %refs_3_.5) | copy-start | bytes 9220
  40.9 11.3 %collective-permute-start.4 = (bf16[8,3,96,128]{3,2,1,0:T(8,128)(2,1)S(1)}, bf16[8,3,96,128]{3,2,1,0:T(8,128)(2,1)S(1)}, u32[]{:S(2)}, u32[]{:S(2)}) collective-permute-start(bf16[8,3,96,128]{3,2,1,0:T(8,128)(2,1)S(1)} %get-tuple-element.23), channel_id=1, source_target_pairs={{0,1},{1,0},{2,3},{3,2},{4,5},{5,4},{6,7},{7,6},{8,9},{9,8},{10,11... | collective-permute-start | bytes 1769480 | tf_op jit(solution)/shard_map/ppermute | solution.py:190
  47.9 9.7 %collective-permute-start.7 = (bf16[8,3,96,128]{3,2,1,0:T(8,128)(2,1)S(1)}, bf16[8,3,96,128]{3,2,1,0:T(8,128)(2,1)S(1)}, u32[]{:S(2)}, u32[]{:S(2)}) collective-permute-start(bf16[8,3,96,128]{3,2,1,0:T(8,128)(2,1)S(1)} %get-tuple-element.26), channel_id=1, source_target_pairs={{0,1},{1,0},{2,3},{3,2},{4,5},{5,4},{6,7},{7,6},{8,9},{9,8},{10,11... | collective-permute-start | bytes 1769480 | tf_op jit(solution)/shard_map/ppermute | solution.py:190
  49.3 8.2 %collective-permute-start.5 = (bf16[4,3,96,128]{3,2,1,0:T(8,128)(2,1)S(1)}, bf16[4,3,96,128]{3,2,1,0:T(8,128)(2,1)S(1)}, u32[]{:S(2)}, u32[]{:S(2)}) collective-permute-start(bf16[4,3,96,128]{3,2,1,0:T(8,128)(2,1)S(1)} %get-tuple-element.32), channel_id=1, source_target_pairs={{2,4},{4,2},{6,8},{8,6},{10,12},{12,10},{14,16},{16,14},{18,20},{2... | collective-permute-start | bytes 884744 | tf_op jit(solution)/shard_map/ppermute | solution.py:146
  51.4 9.7 %collective-permute-start.8 = (bf16[4,3,96,128]{3,2,1,0:T(8,128)(2,1)S(1)}, bf16[4,3,96,128]{3,2,1,0:T(8,128)(2,1)S(1)}, u32[]{:S(2)}, u32[]{:S(2)}) collective-permute-start(bf16[4,3,96,128]{3,2,1,0:T(8,128)(2,1)S(1)} %get-tuple-element.31), channel_id=1, source_target_pairs={{2,4},{4,2},{6,8},{8,6},{10,12},{12,10},{14,16},{16,14},{18,20},{2... | collective-permute-start | bytes 884744 | tf_op jit(solution)/shard_map/ppermute | solution.py:146
where the time goes:
time: 65.1 us; the launch traced here: 64.8 us
  waiting for transfers between devices  20.9 us (32%)
  Pallas kernels  20 us (31%)
  starting transfers between devices  15.5 us (24%)
  local copies, waits for them, and re-layouts  6.42 us (10%)
  other arithmetic  1.27 us (2%)
  between operations  0.79 us (1%)
    ppermute x5, waiting for transfers between devices, shards(): links = [lax.ppermute(x, 'gy', link_pairs) for x in near_cuts + far_cuts]  20.9 us
    pallas_call x3, Pallas kernels, shards(): pl.pallas_call(functools.partial(velocity_kernel, len(beside), far is Non...  12.5 us
    pallas_call x2, Pallas kernels, smooth(): pl.pallas_call(functools.partial(smooth_kernel, start, block, 4), out_sha...  7.46 us
    ppermute x5, starting transfers between devices, shards(): links = [lax.ppermute(x, 'gy', link_pairs) for x in near_cuts + far_cuts]  7.26 us
    dynamic_slice x4, local copies, waits for them, and re-layouts, cut(): lax.dynamic_slice(fields, (start, 0, row, block * lanes), (count, parts,...  6.38 us
    ppermute x1, starting transfers between devices, shards(): lax.ppermute(cut(fields, 0, steps, core_row, near_block), 'gy', core_pairs)  5.57 us
    ppermute x2, starting transfers between devices, shards(): near_halo = [lax.ppermute(edge, 'gz', near_pairs) for _, edge in near]  2.64 us
  transfers between devices with their start and end apart: 9, of which 2 were waited for; matrix products, arithmetic and copies ran while one was open for 9% of the time, Pallas kernels for 25%

commit v1 on v0

v1 whole, which is shorter than its diff:
```python
import functools
import math

import jax
import jax.numpy as jnp
from jax import lax
from jax.experimental import pallas as pl
from jax.experimental.pallas import tpu as pltpu
from jax.sharding import PartitionSpec as P

HALF = 96


VMEM = pl.BlockSpec(memory_space=pltpu.VMEM)
GRANT = 12 * 2**20


def pairs(count, first, closed):
    found = []
    for low in range(first, count, 2):
        if low + 1 < count or closed:
            high = (low + 1) % count
            found += [(low, high), (high, low)]
    return found


def chunks_of(steps):
    ends = [max(1, steps // 4), max(1, (5 * steps) // 8), steps]
    near = [(a, b - a) for a, b in zip([0] + ends, ends) if b > a]
    start, count = near[-1]
    last = count // 3
    far = near[:-1] + ([(start, count - last), (start + count - last, last)] if last else near[-1:])
    return near, far


def parity(axis):
    return lax.axis_index(axis) % 2


def half_of(block):
    odd = parity("gz")
    return odd if block else 1 - odd


def taps(lag):
    scale = HALF * 1.0
    offsets = lax.broadcasted_iota(jnp.int32, (8, 2 * HALF + 1), 1) - HALF
    offsets = offsets.astype(jnp.float32)
    kernel = jnp.exp(-math.pi * offsets * offsets / (2.0 * scale * scale))
    norm = jnp.sqrt(jnp.sum(kernel * kernel, axis=1, keepdims=True))[:1, :1]
    lag = lag.astype(jnp.float32)
    value = jnp.exp(-math.pi * lag * lag / (2.0 * scale * scale)) / norm
    return jnp.where(jnp.abs(lag) <= HALF, value, jnp.zeros_like(value)).astype(jnp.bfloat16)


def bands_kernel(weights, walls):
    rows = weights.shape[0]
    before, after = -HALF, rows
    odd = parity("gy")
    i = lax.broadcasted_iota(jnp.int32, weights.shape, 0)
    j = lax.broadcasted_iota(jnp.int32, weights.shape, 1)
    at_core = j + jnp.where(odd == 1, before, after)
    at_link = j - HALF - rows + jnp.where(odd == 1, after, before)
    at = jnp.where(j < HALF, at_core, jnp.where(j < HALF + rows, j - HALF, at_link))
    weights[...] = taps(at - i)

    cols = walls.shape[1]
    lanes = cols // 2
    odd = parity("gz")
    j = lax.broadcasted_iota(jnp.int32, walls.shape, 0)
    m = lax.broadcasted_iota(jnp.int32, walls.shape, 1)
    at_far = j + half_of(1) * lanes
    at_near = j - lanes + half_of(0) * lanes
    at_near_halo = j - cols + jnp.where(odd == 1, -HALF, cols)
    at_far_halo = j - cols - HALF + jnp.where(odd == 1, cols, -HALF)
    at = jnp.where(j < cols + HALF, at_near_halo, at_far_halo)
    at = jnp.where(j < lanes, at_far, jnp.where(j < cols, at_near, at))
    walls[...] = taps(at - m)


def pack_kernel(cuts, own, *outs):
    rows = own.shape[2]
    for (start, count, side, block), out in zip(cuts, outs):
        lanes = out.shape[3]
        odd = parity("gy")
        row = pl.multiple_of((1 - odd if side else odd) * (rows - HALF), math.gcd(rows - HALF, 128))
        lane = pl.multiple_of(half_of(block) * lanes, lanes)
        for t in range(count):
            for c in range(own.shape[1]):
                out[t, c] = own[start + t, c, pl.ds(row, HALF), pl.ds(lane, lanes)]


def span_product(weights, core, own, link):
    planes = [jnp.concatenate([core[p], own[p], link[p]], axis=0) for p in range(len(own))]
    return jnp.dot(weights, jnp.concatenate(planes, axis=1), preferred_element_type=jnp.float32)


def smooth_planes(block, start, first, count, weights, own, core, link):
    parts, lanes = own.shape[1], core.shape[3]
    lane = pl.multiple_of(half_of(block) * lanes, lanes)
    index = [(t, c) for t in range(count) for c in range(parts)]
    product = span_product(
        weights[...],
        [core[start + first + t, c] for t, c in index],
        [own[start + first + t, c, :, pl.ds(lane, lanes)] for t, c in index],
        [link[first + t, c] for t, c in index],
    ).astype(own.dtype)
    return {i: product[:, p * lanes : (p + 1) * lanes] for p, i in enumerate(index)}


def smooth_kernel(start, block, per, weights, own, core, link, out, edge):
    steps = out.shape[0]
    width = edge.shape[2]
    for first in range(0, steps, per):
        planes = smooth_planes(block, start, first, min(per, steps - first), weights, own, core, link)
        upper = half_of(block)
        for (t, c), plane in planes.items():
            out[first + t, c] = plane
        turned = {i: plane.T for i, plane in planes.items()}

        @pl.when(upper == 1)
        def _():
            for (t, c), plane in turned.items():
                edge[first + t, c] = plane[plane.shape[0] - width :, :]

        @pl.when(upper == 0)
        def _():
            for (t, c), plane in turned.items():
                edge[first + t, c] = plane[:width, :]


def velocity_kernel(halos, raw, start, near_first, per, weights, walls, *refs):
    (decay, mean, diag, off, before, own, core, link, near), rest = refs[:9], refs[9:]
    beside = rest[:halos]
    velocity, state = rest[-2:]
    parts, rows = own.shape[1:3]

    @pl.when(pl.program_id(0) == 0)
    def _():
        state[...] = before[...]

    first = pl.program_id(0) * per
    index = [(t, c) for t in range(per) for c in range(parts)]
    if raw:
        far = smooth_planes(1, start, first, per, weights, own, core, link)
    else:
        far = {(t, c): own[first + t, c] for t, c in index}
    offsets = [near_first, 0]
    cells = []
    for t, c in index:
        sides = [ref[offset + first + t, c].T for ref, offset in zip(beside, offsets)]
        cells.append(jnp.concatenate([far[t, c], near[near_first + first + t, c]] + sides, axis=1))
    filtered = jnp.dot(jnp.concatenate(cells, axis=0), walls[...], preferred_element_type=jnp.float32)
    keep = decay[...]
    fresh = jnp.sqrt(1.0 - keep * keep)
    line = lambda x, c: x[c : c + 1, :]
    u, d, o = mean[...], diag[...], off[...]
    now = [state[c] for c in range(parts)]
    for t in range(per):
        for c in range(parts):
            p = t * parts + c
            now[c] = line(keep, c) * now[c] + line(fresh, c) * filtered[p * rows : (p + 1) * rows]
        velocity[t, 0] = line(u, 0) + line(d, 0) * now[0]
        velocity[t, 1] = line(u, 1) + line(o, 0) * now[0] + line(d, 1) * now[1]
        velocity[t, 2] = line(u, 2) + line(o, 1) * now[0] + line(o, 2) * now[1] + line(d, 2) * now[2]
    for c in range(parts):
        state[c] = now[c]


def shards(random_fields, previous, decay, mean_flow, lund_diag, lund_off):
    steps, parts, rows, cols = random_fields.shape
    lanes = cols // 2
    span_count = lax.axis_size("gy")
    wall_count = lax.axis_size("gz")
    kind = random_fields.dtype
    params = pltpu.CompilerParams(vmem_limit_bytes=GRANT)

    core_pairs = pairs(span_count, 0, True)
    link_pairs = pairs(span_count, 1, True)
    near_pairs = pairs(wall_count, 0, False)
    far_pairs = pairs(wall_count, 1, False)
    near_chunks, far_chunks = chunks_of(steps)

    start, count = near_chunks[0]
    first_cut = lax.dynamic_slice(
        random_fields,
        (start, 0, parity("gy") * (rows - HALF), half_of(0) * lanes),
        (count, parts, HALF, lanes),
    )
    own, first_cut = lax.optimization_barrier((random_fields, first_cut))

    cuts = [(0, steps, 1, 0)] + [(s, n, 0, 0) for s, n in near_chunks[1:]]
    cuts += [(s, n, 0, 1) for s, n in far_chunks] + [(0, steps, 1, 1)]
    packed = pl.pallas_call(
        functools.partial(pack_kernel, cuts),
        out_shape=[jax.ShapeDtypeStruct((n, parts, HALF, lanes), kind) for _, n, _, _ in cuts],
        in_specs=[VMEM],
        out_specs=[VMEM] * len(cuts),
        compiler_params=params,
        name="pack",
    )(own)
    near_core = lax.ppermute(packed[0], "gy", core_pairs)
    far_core = lax.ppermute(packed[-1], "gy", core_pairs)
    links = [lax.ppermute(x, "gy", link_pairs) for x in [first_cut, *packed[1:-1]]]
    near_link, far_link = links[: len(near_chunks)], links[len(near_chunks) :]

    depth = cols + HALF * (bool(near_pairs) + bool(far_pairs))
    weights, walls = pl.pallas_call(
        bands_kernel,
        out_shape=(
            jax.ShapeDtypeStruct((rows, rows + 2 * HALF), kind),
            jax.ShapeDtypeStruct((depth, cols), kind),
        ),
        out_specs=(VMEM, VMEM),
        compiler_params=params,
        name="bands",
    )()

    def smooth(start, count, block, core, link):
        return pl.pallas_call(
            functools.partial(smooth_kernel, start, block, 3),
            out_shape=(
                jax.ShapeDtypeStruct((count, parts, rows, lanes), kind),
                jax.ShapeDtypeStruct((count, parts, HALF, rows), kind),
            ),
            in_specs=[VMEM] * 4,
            out_specs=(VMEM, VMEM),
            compiler_params=params,
            cost_estimate=pl.CostEstimate(
                flops=2 * count * parts * rows * lanes * (rows + 2 * HALF),
                bytes_accessed=4 * count * parts * lanes * (rows + HALF),
                transcendentals=0,
            ),
            name="smooth",
        )(weights, own, core, link)

    near = [smooth(s, n, 0, near_core, link) for (s, n), link in zip(near_chunks, near_link)]
    near_halo, far_halo, far = [], [], None
    if near_pairs:
        near_halo = [lax.ppermute(edge, "gz", near_pairs) for _, edge in near]
    if far_pairs:
        far = [smooth(s, n, 1, far_core, link) for (s, n), link in zip(far_chunks, far_link)]
        far_halo = [lax.ppermute(edge, "gz", far_pairs) for _, edge in far]

    velocity, state = None, previous
    for k, (s, n) in enumerate(far_chunks):
        source = max(q for q, (first, _) in enumerate(near_chunks) if first <= s)
        per = math.gcd(math.gcd(n, s), 2)
        operands = [weights, walls, decay, mean_flow, lund_diag, lund_off, state]
        operands += [own if far is None else far[k][0], far_core, far_link[k], near[source][0]]
        beside = near_halo[source : source + 1] + far_halo[k : k + 1]
        operands += beside
        specs = [VMEM] * len(operands)
        aliases = {}
        if velocity is not None:
            aliases = {len(operands): 0}
            operands.append(velocity)
            specs.append(pl.BlockSpec(memory_space=pl.ANY))
        velocity, state = pl.pallas_call(
            functools.partial(velocity_kernel, len(beside), far is None, s, s - near_chunks[source][0], per),
            out_shape=(
                jax.ShapeDtypeStruct((steps, parts, rows, cols), jnp.float32),
                jax.ShapeDtypeStruct(previous.shape, jnp.float32),
            ),
            grid=(n // per,),
            in_specs=specs,
            out_specs=(
                pl.BlockSpec((per, parts, rows, cols), functools.partial(lambda o, t: (o + t, 0, 0, 0), s // per)),
                VMEM,
            ),
            input_output_aliases=aliases,
            compiler_params=params,
            cost_estimate=pl.CostEstimate(
                flops=2 * n * parts * rows * (lanes * (rows + 2 * HALF) + cols * depth),
                bytes_accessed=n * parts * rows * (4 * cols + 10 * lanes),
                transcendentals=0,
            ),
            name="velocity",
        )(*operands)
    return velocity


def solution(mesh):
    return jax.shard_map(
        shards,
        mesh=mesh,
        in_specs=(
            P(None, None, "gy", "gz"),
            P(None, "gy", "gz"),
            P(None, "gz"),
            P(None, "gz"),
            P(None, "gz"),
            P(None, "gz"),
        ),
        out_specs=P(None, None, "gy", "gz"),
        check_vma=False,
    )
```

time: 65.1 us -> 70.3 us (1.080)
  waiting for transfers between devices: 20.9 us -> 37.4 us
  Pallas kernels: 20 us -> 12.7 us
  local copies, waits for them, and re-layouts: 6.42 us -> 2.9 us
  starting transfers between devices: 15.5 us -> 17 us
  other arithmetic: 1.27 us -> 0 us
    ppermute x7 -> x9, waiting for transfers between devices: 20.9 us -> 32.7 us  [the longest x7 32.7 us: shards(): lax.ppermute(x, 'gy', link_pairs)]
    dynamic_slice x4 -> x1, local copies, waits for them, and re-layouts: 6.38 us -> 0.98 us  [shards(): lax.dynamic_slice(random_fields, (start, 0, parity('gy') * (rows - HALF),...]
    ppermute x2 -> x3, waiting for transfers between devices: 0.01 us -> 4.76 us  [shards(): near_halo = [lax.ppermute(edge, 'gz', near_pairs) for _, edge in near]]
    pallas_call x2 -> x5, Pallas kernels: 7.46 us -> 3.4 us  [the longest x3 2.28 us: smooth(): pl.pallas_call(functools.partial(smooth_kernel, start, block, 3), out_sha...]
    pallas_call x3 -> x4, Pallas kernels: 12.5 us -> 9.31 us  [shards(): pl.pallas_call(functools.partial(velocity_kernel, len(beside), far is Non...]
    unnamed x12 -> x14, local copies, waits for them, and re-layouts: 0.04 us -> 1.92 us
    ppermute x2 -> x3, starting transfers between devices: 2.64 us -> 4.01 us  [shards(): near_halo = [lax.ppermute(edge, 'gz', near_pairs) for _, edge in near]]
    ppermute x7 -> x9, starting transfers between devices: 12.8 us -> 13 us  [the longest x7 12.4 us: shards(): lax.ppermute(x, 'gy', link_pairs)]
  transfers between devices with their start and end apart: 9 -> 12, of which waited for: 2 -> 5; matrix products, arithmetic and copies ran while one was open for 9% -> 0% of each run, Pallas kernels for 25% -> 15%
where the time goes in v1:
time: 70.3 us; the launch traced here: 70.1 us
  waiting for transfers between devices  37.4 us (53%)
  starting transfers between devices  17 us (24%)
  Pallas kernels  12.7 us (18%)
  local copies, waits for them, and re-layouts  2.9 us (4%)
    ppermute x7, waiting for transfers between devices, shards(): lax.ppermute(x, 'gy', link_pairs)  32.7 us
    ppermute x7, starting transfers between devices, shards(): lax.ppermute(x, 'gy', link_pairs)  12.4 us
    pallas_call x4, Pallas kernels, shards(): pl.pallas_call(functools.partial(velocity_kernel, len(beside), far is Non...  9.31 us
    ppermute x3, waiting for transfers between devices, shards(): near_halo = [lax.ppermute(edge, 'gz', near_pairs) for _, edge in near]  4.76 us
    ppermute x3, starting transfers between devices, shards(): near_halo = [lax.ppermute(edge, 'gz', near_pairs) for _, edge in near]  4.01 us
    pallas_call x3, Pallas kernels, smooth(): pl.pallas_call(functools.partial(smooth_kernel, start, block, 3), out_sha...  2.28 us
    unnamed x14, local copies, waits for them, and re-layouts  1.92 us
  transfers between devices with their start and end apart: 12, of which 5 were waited for; matrix products, arithmetic and copies ran while one was open for 0% of the time, Pallas kernels for 15%

profile of v1, /device:TPU:1, one launch (start us, length us, event | category | flops | bytes accessed | tf_op | source)
XLA Modules:
  0.0 70.1 jit_solution(2681053252051218902)
XLA Ops:
  0.0 1.0 %constant_dynamic-slice_fusion = bf16[4,3,96,128]{3,2,1,0:T(8,128)(2,1)S(1)} fusion(bf16[16,3,128,256]{3,2,1,0:T(8,128)(2,1)} %refs_5_.3, s32[]{:T(128)S(6)} %select_n.18, s32[]{:T(128)S(6)} %select_n.20), kind=kLoop, calls=%fused_computation | loop fusion | bytes 589832 | tf_op jit(solution)/shard_map/dynamic_slice | solution.py:185
  1.0 0.0 copy-start
  1.0 1.9 %copy-done = bf16[16,3,128,256]{3,2,1,0:T(8,128)(2,1)S(1)} copy-done((bf16[16,3,128,256]{3,2,1,0:T(8,128)(2,1)S(1)}, bf16[16,3,128,256]{3,2,1,0:T(8,128)(2,1)}, u32[]{:S(2)}) %copy-start) | copy-done | bytes 3145752
  2.9 0.0 copy-start.1
  2.9 0.8 %pack.1 = (bf16[16,3,96,128]{3,2,1,0:T(8,128)(2,1)S(1)}, bf16[6,3,96,128]{3,2,1,0:T(8,128)(2,1)S(1)}, bf16[6,3,96,128]{3,2,1,0:T(8,128)(2,1)S(1)}, bf16[4,3,96,1...) custom-call(bf16[16,3,128,256]{3,2,1,0:T(8,128)(2,1)S(1)} %copy-done), custom_call_target="tpu_custom_call" | custom-call | tf_op jit(solution)/shard_map/pack/pallas_call | solution.py:194
  3.6 0.1 collective-permute-start.2
  3.7 0.5 collective-permute-start
  4.2 2.6 %collective-permute-start.6 = (bf16[6,3,96,128]{3,2,1,0:T(8,128)(2,1)S(1)}, bf16[6,3,96,128]{3,2,1,0:T(8,128)(2,1)S(1)}, u32[]{:S(2)}, u32[]{:S(2)}) collective-permute-start(bf16[6,3,96,128]{3,2,1,0:T(8,128)(2,1)S(1)} %get-tuple-element.41), channel_id=1, source_target_pairs={{2,4},{4,2},{6,8},{8,6},{10,12},{12,10},{14,16},{16,14},{18,20},{2... | collective-permute-start | bytes 1327112 | tf_op jit(solution)/shard_map/ppermute | solution.py:204
  6.8 0.0 collective-permute-start.9
  6.9 1.7 %collective-permute-start.3 = (bf16[4,3,96,128]{3,2,1,0:T(8,128)(2,1)S(1)}, bf16[4,3,96,128]{3,2,1,0:T(8,128)(2,1)S(1)}, u32[]{:S(2)}, u32[]{:S(2)}) collective-permute-start(bf16[4,3,96,128]{3,2,1,0:T(8,128)(2,1)S(1)} %constant_dynamic-slice_fusion), channel_id=1, source_target_pairs={{2,4},{4,2},{6,8},{8,6},{10,12},{12,10},{14,16},{16,14},{18,20},{2... | collective-permute-start | bytes 884744 | tf_op jit(solution)/shard_map/ppermute | solution.py:204
  8.6 27.2 %collective-permute-done.6.link = bf16[6,3,96,128]{3,2,1,0:T(8,128)(2,1)S(1)} collective-permute-done((bf16[6,3,96,128]{3,2,1,0:T(8,128)(2,1)S(1)}, bf16[6,3,96,128]{3,2,1,0:T(8,128)(2,1)S(1)}, u32[]{:S(2)}, u32[]{:S(2)}) %collective-permute-start.6) | collective-permute-done | bytes 442400 | tf_op jit(solution)/shard_map/ppermute | solution.py:204
  35.8 2.5 %collective-permute-start.1 = (bf16[4,3,96,128]{3,2,1,0:T(8,128)(2,1)S(1)}, bf16[4,3,96,128]{3,2,1,0:T(8,128)(2,1)S(1)}, u32[]{:S(2)}, u32[]{:S(2)}) collective-permute-start(bf16[4,3,96,128]{3,2,1,0:T(8,128)(2,1)S(1)} %get-tuple-element.34), channel_id=1, source_target_pairs={{2,4},{4,2},{6,8},{8,6},{10,12},{12,10},{14,16},{16,14},{18,20},{2... | collective-permute-start | bytes 884744 | tf_op jit(solution)/shard_map/ppermute | solution.py:204
  38.3 0.4 bands.1
  38.6 0.0 collective-permute-done.2.core
  38.6 0.1 collective-permute-start.5
  38.7 0.0 copy-done.1
  38.7 0.8 %smooth.4 = (bf16[6,3,128,128]{3,2,1,0:T(8,128)(2,1)S(1)}, bf16[6,3,96,128]{3,2,1,0:T(8,128)(2,1)S(1)}) custom-call(bf16[128,320]{1,0:T(8,128)(2,1)S(1)} %get-tuple-element.30.weights, bf16[16,3,128,256]{3,2,1,0:T(8,128)(2,1)S(1)} %copy-done.1, bf16[16,3,96,128]{3,2,1,0:T(8,128)(2,1)S(1)} %collective-permute-done.2.core, ...), custom_call_target="tpu_custom_call" | custom-call | flops 188743680 | bytes 2064384 | tf_op jit(solution)/shard_map/smooth/pallas_call | solution.py:220
  39.5 2.6 %collective-permute-done.9.link = bf16[6,3,96,128]{3,2,1,0:T(8,128)(2,1)S(1)} collective-permute-done((bf16[6,3,96,128]{3,2,1,0:T(8,128)(2,1)S(1)}, bf16[6,3,96,128]{3,2,1,0:T(8,128)(2,1)S(1)}, u32[]{:S(2)}, u32[]{:S(2)}) %collective-permute-start.9) | collective-permute-done | bytes 442400 | tf_op jit(solution)/shard_map/ppermute | solution.py:204
  42.1 1.2 %collective-permute-start.7 = (bf16[6,3,96,128]{3,2,1,0:T(8,128)(2,1)S(1)}, bf16[6,3,96,128]{3,2,1,0:T(8,128)(2,1)S(1)}, u32[]{:S(2)}, u32[]{:S(2)}) collective-permute-start(bf16[6,3,96,128]{3,2,1,0:T(8,128)(2,1)S(1)} %get-tuple-element.43), channel_id=1, source_target_pairs={{0,1},{1,0},{2,3},{3,2},{4,5},{5,4},{6,7},{7,6},{8,9},{9,8},{10,11... | collective-permute-start | bytes 1327112 | tf_op jit(solution)/shard_map/ppermute | solution.py:240
  43.3 0.8 %smooth.5 = (bf16[6,3,128,128]{3,2,1,0:T(8,128)(2,1)S(1)}, bf16[6,3,96,128]{3,2,1,0:T(8,128)(2,1)S(1)}) custom-call(bf16[128,320]{1,0:T(8,128)(2,1)S(1)} %get-tuple-element.30.weights, bf16[16,3,128,256]{3,2,1,0:T(8,128)(2,1)S(1)} %copy-done.1, bf16[16,3,96,128]{3,2,1,0:T(8,128)(2,1)S(1)} %collective-permute-done.2.core, ...), custom_call_target="tpu_custom_call" | custom-call | flops 188743680 | bytes 2064384 | tf_op jit(solution)/shard_map/smooth/pallas_call | solution.py:220
  44.1 0.0 copy-start.2
  44.1 0.0 copy-start.3
  44.1 0.0 copy-start.4
  44.2 0.0 copy-start.5
  44.2 0.0 copy-start.6
  44.2 1.8 %collective-permute-done.3.link = bf16[4,3,96,128]{3,2,1,0:T(8,128)(2,1)S(1)} collective-permute-done((bf16[4,3,96,128]{3,2,1,0:T(8,128)(2,1)S(1)}, bf16[4,3,96,128]{3,2,1,0:T(8,128)(2,1)S(1)}, u32[]{:S(2)}, u32[]{:S(2)}) %collective-permute-start.3) | collective-permute-done | bytes 294944 | tf_op jit(solution)/shard_map/ppermute | solution.py:204
  46.0 1.4 %collective-permute-start.10 = (bf16[6,3,96,128]{3,2,1,0:T(8,128)(2,1)S(1)}, bf16[6,3,96,128]{3,2,1,0:T(8,128)(2,1)S(1)}, u32[]{:S(2)}, u32[]{:S(2)}) collective-permute-start(bf16[6,3,96,128]{3,2,1,0:T(8,128)(2,1)S(1)} %get-tuple-element.49), channel_id=1, source_target_pairs={{0,1},{1,0},{2,3},{3,2},{4,5},{5,4},{6,7},{7,6},{8,9},{9,8},{10,11... | collective-permute-start | bytes 1327112 | tf_op jit(solution)/shard_map/ppermute | solution.py:240
  47.4 0.7 smooth.3
  48.1 1.1 %collective-permute-done.1.refs_7_ = bf16[4,3,96,128]{3,2,1,0:T(8,128)(2,1)S(1)} collective-permute-done((bf16[4,3,96,128]{3,2,1,0:T(8,128)(2,1)S(1)}, bf16[4,3,96,128]{3,2,1,0:T(8,128)(2,1)S(1)}, u32[]{:S(2)}, u32[]{:S(2)}) %collective-permute-start.1) | collective-permute-done | bytes 294944 | tf_op jit(solution)/shard_map/ppermute | solution.py:204
  49.2 1.4 %collective-permute-start.4 = (bf16[4,3,96,128]{3,2,1,0:T(8,128)(2,1)S(1)}, bf16[4,3,96,128]{3,2,1,0:T(8,128)(2,1)S(1)}, u32[]{:S(2)}, u32[]{:S(2)}) collective-permute-start(bf16[4,3,96,128]{3,2,1,0:T(8,128)(2,1)S(1)} %get-tuple-element.38), channel_id=1, source_target_pairs={{0,1},{1,0},{2,3},{3,2},{4,5},{5,4},{6,7},{7,6},{8,9},{9,8},{10,11... | collective-permute-start | bytes 884744 | tf_op jit(solution)/shard_map/ppermute | solution.py:240
  50.6 0.0 collective-permute-done.refs_6_
  50.6 1.8 %collective-permute-start.8 = (bf16[4,3,96,128]{3,2,1,0:T(8,128)(2,1)S(1)}, bf16[4,3,96,128]{3,2,1,0:T(8,128)(2,1)S(1)}, u32[]{:S(2)}, u32[]{:S(2)}) collective-permute-start(bf16[4,3,96,128]{3,2,1,0:T(8,128)(2,1)S(1)} %get-tuple-element.46), channel_id=1, source_target_pairs={{2,4},{4,2},{6,8},{8,6},{10,12},{12,10},{14,16},{16,14},{18,20},{2... | collective-permute-start | bytes 884744 | tf_op jit(solution)/shard_map/ppermute | solution.py:204
  52.4 4.8 %collective-permute-done.4.refs_9_ = bf16[4,3,96,128]{3,2,1,0:T(8,128)(2,1)S(1)} collective-permute-done((bf16[4,3,96,128]{3,2,1,0:T(8,128)(2,1)S(1)}, bf16[4,3,96,128]{3,2,1,0:T(8,128)(2,1)S(1)}, u32[]{:S(2)}, u32[]{:S(2)}) %collective-permute-start.4) | collective-permute-done | bytes 294944 | tf_op jit(solution)/shard_map/ppermute | solution.py:240
  57.2 3.6 %collective-permute-start.11 = (bf16[2,3,96,128]{3,2,1,0:T(8,128)(2,1)S(1)}, bf16[2,3,96,128]{3,2,1,0:T(8,128)(2,1)S(1)}, u32[]{:S(2)}, u32[]{:S(2)}) collective-permute-start(bf16[2,3,96,128]{3,2,1,0:T(8,128)(2,1)S(1)} %get-tuple-element.52), channel_id=1, source_target_pairs={{2,4},{4,2},{6,8},{8,6},{10,12},{12,10},{14,16},{16,14},{18,20},{2... | collective-permute-start | bytes 442376 | tf_op jit(solution)/shard_map/ppermute | solution.py:204
  60.8 0.0 copy-done.2
  60.8 0.0 copy-done.3
  60.8 0.0 copy-done.4
  60.8 0.0 copy-done.5
  60.8 0.0 copy-done.6
  60.8 2.3 %velocity.4 = (f32[16,3,128,256]{3,2,1,0:T(8,128)}, f32[3,128,256]{2,1,0:T(8,128)S(1)}) custom-call(bf16[128,320]{1,0:T(8,128)(2,1)S(1)} %get-tuple-element.30.weights, bf16[352,256]{1,0:T(8,128)(2,1)S(1)} %get-tuple-element.31.walls, f32[3,256]{1,0:T(4,128)S(1)} %copy-done.3, f32[3,256]{1,0:T(4,128)S(1)} %copy-done.4, f32[3,256]{1,0:T(4,128)S(1)} %copy-done.5, ...), custom_call_target="tpu_custom_call" | custom-call | flops 402653184 | bytes 3538944 | tf_op jit(solution)/shard_map/velocity/pallas_call | solution.py:259
  63.1 0.0 collective-permute-done.5.refs_7_
  63.1 0.0 collective-permute-done.7.refs_9_
  63.1 3.1 %velocity.5 = (f32[16,3,128,256]{3,2,1,0:T(8,128)}, f32[3,128,256]{2,1,0:T(8,128)S(1)}) custom-call(bf16[128,320]{1,0:T(8,128)(2,1)S(1)} %get-tuple-element.30.weights, bf16[352,256]{1,0:T(8,128)(2,1)S(1)} %get-tuple-element.31.walls, f32[3,256]{1,0:T(4,128)S(1)} %copy-done.3, f32[3,256]{1,0:T(4,128)S(1)} %copy-done.4, ...), custom_call_target="tpu_custom_call", output_to_operand_aliasing={{0}: (12, {})} | custom-call | flops 603979776 | bytes 5308416 | tf_op jit(solution)/shard_map/velocity/pallas_call | solution.py:259
  66.2 0.0 collective-permute-done.8.refs_7_
  66.2 0.0 collective-permute-done.10.refs_9_
  66.2 2.3 %velocity.6 = (f32[16,3,128,256]{3,2,1,0:T(8,128)}, f32[3,128,256]{2,1,0:T(8,128)S(1)}) custom-call(bf16[128,320]{1,0:T(8,128)(2,1)S(1)} %get-tuple-element.30.weights, bf16[352,256]{1,0:T(8,128)(2,1)S(1)} %get-tuple-element.31.walls, f32[3,256]{1,0:T(4,128)S(1)} %copy-done.3, f32[3,256]{1,0:T(4,128)S(1)} %copy-done.4, ...), custom_call_target="tpu_custom_call", output_to_operand_aliasing={{0}: (12, {})} | custom-call | flops 402653184 | bytes 3538944 | tf_op jit(solution)/shard_map/velocity/pallas_call | solution.py:259
  68.5 0.0 collective-permute-done.11.refs_7_
  68.5 1.7 %velocity.7 = (f32[16,3,128,256]{3,2,1,0:T(8,128)}, f32[3,128,256]{2,1,0:T(8,128)}) custom-call(bf16[128,320]{1,0:T(8,128)(2,1)S(1)} %get-tuple-element.30.weights, bf16[352,256]{1,0:T(8,128)(2,1)S(1)} %get-tuple-element.31.walls, f32[3,256]{1,0:T(4,128)S(1)} %copy-done.3, f32[3,256]{1,0:T(4,128)S(1)} %copy-done.4, ...), custom_call_target="tpu_custom_call", output_to_operand_aliasing={{0}: (12, {})} | custom-call | flops 201326592 | bytes 1769472 | tf_op jit(solution)/shard_map/velocity/pallas_call | solution.py:259
Async XLA Ops:
  1.0 1.9 %copy-start = (bf16[16,3,128,256]{3,2,1,0:T(8,128)(2,1)S(1)}, bf16[16,3,128,256]{3,2,1,0:T(8,128)(2,1)}, u32[]{:S(2)}) copy-start(bf16[16,3,128,256]{3,2,1,0:T(8,128)(2,1)} %refs_5_.3) | copy-start | bytes 9437188
  2.9 35.8 %copy-start.1 = (bf16[16,3,128,256]{3,2,1,0:T(8,128)(2,1)S(1)}, bf16[16,3,128,256]{3,2,1,0:T(8,128)(2,1)}, u32[]{:S(2)}) copy-start(bf16[16,3,128,256]{3,2,1,0:T(8,128)(2,1)} %refs_5_.3) | copy-start | bytes 9437188
  3.6 35.0 %collective-permute-start.2 = (bf16[16,3,96,128]{3,2,1,0:T(8,128)(2,1)S(1)}, bf16[16,3,96,128]{3,2,1,0:T(8,128)(2,1)S(1)}, u32[]{:S(2)}, u32[]{:S(2)}) collective-permute-start(bf16[16,3,96,128]{3,2,1,0:T(8,128)(2,1)S(1)} %get-tuple-element.35), channel_id=1, source_target_pairs={{0,2},{2,0},{4,6},{6,4},{8,10},{10,8},{12,14},{14,12},{16,18},{18,... | collective-permute-start | bytes 3538952 | tf_op jit(solution)/shard_map/ppermute | solution.py:202
  3.7 46.8 %collective-permute-start = (bf16[16,3,96,128]{3,2,1,0:T(8,128)(2,1)S(1)}, bf16[16,3,96,128]{3,2,1,0:T(8,128)(2,1)S(1)}, u32[]{:S(2)}, u32[]{:S(2)}) collective-permute-start(bf16[16,3,96,128]{3,2,1,0:T(8,128)(2,1)S(1)} %get-tuple-element.33), channel_id=1, source_target_pairs={{0,2},{2,0},{4,6},{6,4},{8,10},{10,8},{12,14},{14,12},{16,18},{18,... | collective-permute-start | bytes 3538952 | tf_op jit(solution)/shard_map/ppermute | solution.py:203
  4.2 31.6 %collective-permute-start.6 = (bf16[6,3,96,128]{3,2,1,0:T(8,128)(2,1)S(1)}, bf16[6,3,96,128]{3,2,1,0:T(8,128)(2,1)S(1)}, u32[]{:S(2)}, u32[]{:S(2)}) collective-permute-start(bf16[6,3,96,128]{3,2,1,0:T(8,128)(2,1)S(1)} %get-tuple-element.41), channel_id=1, source_target_pairs={{2,4},{4,2},{6,8},{8,6},{10,12},{12,10},{14,16},{16,14},{18,20},{2... | collective-permute-start | bytes 1327112 | tf_op jit(solution)/shard_map/ppermute | solution.py:204
  6.8 35.3 %collective-permute-start.9 = (bf16[6,3,96,128]{3,2,1,0:T(8,128)(2,1)S(1)}, bf16[6,3,96,128]{3,2,1,0:T(8,128)(2,1)S(1)}, u32[]{:S(2)}, u32[]{:S(2)}) collective-permute-start(bf16[6,3,96,128]{3,2,1,0:T(8,128)(2,1)S(1)} %get-tuple-element.47), channel_id=1, source_target_pairs={{2,4},{4,2},{6,8},{8,6},{10,12},{12,10},{14,16},{16,14},{18,20},{2... | collective-permute-start | bytes 1327112 | tf_op jit(solution)/shard_map/ppermute | solution.py:204
  6.9 39.1 %collective-permute-start.3 = (bf16[4,3,96,128]{3,2,1,0:T(8,128)(2,1)S(1)}, bf16[4,3,96,128]{3,2,1,0:T(8,128)(2,1)S(1)}, u32[]{:S(2)}, u32[]{:S(2)}) collective-permute-start(bf16[4,3,96,128]{3,2,1,0:T(8,128)(2,1)S(1)} %constant_dynamic-slice_fusion), channel_id=1, source_target_pairs={{2,4},{4,2},{6,8},{8,6},{10,12},{12,10},{14,16},{16,14},{18,20},{2... | collective-permute-start | bytes 884744 | tf_op jit(solution)/shard_map/ppermute | solution.py:204
  35.8 13.4 %collective-permute-start.1 = (bf16[4,3,96,128]{3,2,1,0:T(8,128)(2,1)S(1)}, bf16[4,3,96,128]{3,2,1,0:T(8,128)(2,1)S(1)}, u32[]{:S(2)}, u32[]{:S(2)}) collective-permute-start(bf16[4,3,96,128]{3,2,1,0:T(8,128)(2,1)S(1)} %get-tuple-element.34), channel_id=1, source_target_pairs={{2,4},{4,2},{6,8},{8,6},{10,12},{12,10},{14,16},{16,14},{18,20},{2... | collective-permute-start | bytes 884744 | tf_op jit(solution)/shard_map/ppermute | solution.py:204
  38.6 24.4 %collective-permute-start.5 = (bf16[6,3,96,128]{3,2,1,0:T(8,128)(2,1)S(1)}, bf16[6,3,96,128]{3,2,1,0:T(8,128)(2,1)S(1)}, u32[]{:S(2)}, u32[]{:S(2)}) collective-permute-start(bf16[6,3,96,128]{3,2,1,0:T(8,128)(2,1)S(1)} %get-tuple-element.40), channel_id=1, source_target_pairs={{2,4},{4,2},{6,8},{8,6},{10,12},{12,10},{14,16},{16,14},{18,20},{2... | collective-permute-start | bytes 1327112 | tf_op jit(solution)/shard_map/ppermute | solution.py:204
  42.1 21.0 %collective-permute-start.7 = (bf16[6,3,96,128]{3,2,1,0:T(8,128)(2,1)S(1)}, bf16[6,3,96,128]{3,2,1,0:T(8,128)(2,1)S(1)}, u32[]{:S(2)}, u32[]{:S(2)}) collective-permute-start(bf16[6,3,96,128]{3,2,1,0:T(8,128)(2,1)S(1)} %get-tuple-element.43), channel_id=1, source_target_pairs={{0,1},{1,0},{2,3},{3,2},{4,5},{5,4},{6,7},{7,6},{8,9},{9,8},{10,11... | collective-permute-start | bytes 1327112 | tf_op jit(solution)/shard_map/ppermute | solution.py:240
  44.1 16.7 %copy-start.2 = (f32[3,128,256]{2,1,0:T(8,128)S(1)}, f32[3,128,256]{2,1,0:T(8,128)}, u32[]{:S(2)}) copy-start(f32[3,128,256]{2,1,0:T(8,128)} %refs_4_.1) | copy-start | bytes 1179652
  44.1 16.7 %copy-start.3 = (f32[3,256]{1,0:T(4,128)S(1)}, f32[3,256]{1,0:T(4,128)}, u32[]{:S(2)}) copy-start(f32[3,256]{1,0:T(4,128)} %refs_0_.7) | copy-start | bytes 9220
  44.1 16.7 %copy-start.4 = (f32[3,256]{1,0:T(4,128)S(1)}, f32[3,256]{1,0:T(4,128)}, u32[]{:S(2)}) copy-start(f32[3,256]{1,0:T(4,128)} %refs_1_.7) | copy-start | bytes 9220
  44.2 16.6 %copy-start.5 = (f32[3,256]{1,0:T(4,128)S(1)}, f32[3,256]{1,0:T(4,128)}, u32[]{:S(2)}) copy-start(f32[3,256]{1,0:T(4,128)} %refs_2_.7) | copy-start | bytes 9220
  44.2 16.6 %copy-start.6 = (f32[3,256]{1,0:T(4,128)S(1)}, f32[3,256]{1,0:T(4,128)}, u32[]{:S(2)}) copy-start(f32[3,256]{1,0:T(4,128)} %refs_3_.7) | copy-start | bytes 9220
  46.0 20.2 %collective-permute-start.10 = (bf16[6,3,96,128]{3,2,1,0:T(8,128)(2,1)S(1)}, bf16[6,3,96,128]{3,2,1,0:T(8,128)(2,1)S(1)}, u32[]{:S(2)}, u32[]{:S(2)}) collective-permute-start(bf16[6,3,96,128]{3,2,1,0:T(8,128)(2,1)S(1)} %get-tuple-element.49), channel_id=1, source_target_pairs={{0,1},{1,0},{2,3},{3,2},{4,5},{5,4},{6,7},{7,6},{8,9},{9,8},{10,11... | collective-permute-start | bytes 1327112 | tf_op jit(solution)/shard_map/ppermute | solution.py:240
  49.2 8.0 %collective-permute-start.4 = (bf16[4,3,96,128]{3,2,1,0:T(8,128)(2,1)S(1)}, bf16[4,3,96,128]{3,2,1,0:T(8,128)(2,1)S(1)}, u32[]{:S(2)}, u32[]{:S(2)}) collective-permute-start(bf16[4,3,96,128]{3,2,1,0:T(8,128)(2,1)S(1)} %get-tuple-element.38), channel_id=1, source_target_pairs={{0,1},{1,0},{2,3},{3,2},{4,5},{5,4},{6,7},{7,6},{8,9},{9,8},{10,11... | collective-permute-start | bytes 884744 | tf_op jit(solution)/shard_map/ppermute | solution.py:240
  50.6 15.6 %collective-permute-start.8 = (bf16[4,3,96,128]{3,2,1,0:T(8,128)(2,1)S(1)}, bf16[4,3,96,128]{3,2,1,0:T(8,128)(2,1)S(1)}, u32[]{:S(2)}, u32[]{:S(2)}) collective-permute-start(bf16[4,3,96,128]{3,2,1,0:T(8,128)(2,1)S(1)} %get-tuple-element.46), channel_id=1, source_target_pairs={{2,4},{4,2},{6,8},{8,6},{10,12},{12,10},{14,16},{16,14},{18,20},{2... | collective-permute-start | bytes 884744 | tf_op jit(solution)/shard_map/ppermute | solution.py:204
  57.2 11.3 %collective-permute-start.11 = (bf16[2,3,96,128]{3,2,1,0:T(8,128)(2,1)S(1)}, bf16[2,3,96,128]{3,2,1,0:T(8,128)(2,1)S(1)}, u32[]{:S(2)}, u32[]{:S(2)}) collective-permute-start(bf16[2,3,96,128]{3,2,1,0:T(8,128)(2,1)S(1)} %get-tuple-element.52), channel_id=1, source_target_pairs={{2,4},{4,2},{6,8},{8,6},{10,12},{12,10},{14,16},{16,14},{18,20},{2... | collective-permute-start | bytes 442376 | tf_op jit(solution)/shard_map/ppermute | solution.py:204

commit v2 on v1

--- a/solution.py
+++ b/solution.py
@@ -25,12 +25,9 @@
 
 
 def chunks_of(steps):
-    ends = [max(1, steps // 4), max(1, (5 * steps) // 8), steps]
-    near = [(a, b - a) for a, b in zip([0] + ends, ends) if b > a]
-    start, count = near[-1]
-    last = count // 3
-    far = near[:-1] + ([(start, count - last), (start + count - last, last)] if last else near[-1:])
-    return near, far
+    cut = lambda ends: [(a, b - a) for a, b in zip([0] + ends, ends)]
+    sixteenths = lambda *parts: sorted({max(1, p * steps // 16) for p in parts})
+    return cut(sixteenths(3, 8, 12, 16)), cut(sorted({*sixteenths(8, 12, 16), max(1, steps - 1)}))
 
 
 def parity(axis):
@@ -129,42 +126,60 @@
                 edge[first + t, c] = plane[:width, :]
 
 
-def velocity_kernel(halos, raw, start, near_first, per, weights, walls, *refs):
-    (decay, mean, diag, off, before, own, core, link, near), rest = refs[:9], refs[9:]
-    beside = rest[:halos]
-    velocity, state = rest[-2:]
+def velocity_kernel(chunk, sources, raw, halos, kept, last, *refs):
+    start, count = chunk
+    (weights, walls, decay, mean, diag, off, before, own, core, link), rest = refs[:10], refs[10:]
+    near, rest = rest[: len(sources)], rest[len(sources) :]
+    near_halo, rest = (rest[: len(sources)], rest[len(sources) :]) if halos[0] else ((), rest)
+    far_halo, rest = (rest[:1], rest[1:]) if halos[1] else ((), rest)
+    kept_ref, rest = (rest[0], rest[1:]) if kept else (None, rest)
+    if last:
+        velocity, out, sems = rest[-3:]
+    elif kept:
+        velocity, state, out, sems = rest[-4:]
+    else:
+        state, out = rest
+    copies = []
+    if kept:
+        copies.append(pltpu.make_async_copy(kept_ref, velocity.at[pl.ds(*kept)], sems.at[0]))
+        copies[0].start()
+
     parts, rows = own.shape[1:3]
-
-    @pl.when(pl.program_id(0) == 0)
-    def _():
-        state[...] = before[...]
-
-    first = pl.program_id(0) * per
-    index = [(t, c) for t in range(per) for c in range(parts)]
-    if raw:
-        far = smooth_planes(1, start, first, per, weights, own, core, link)
-    else:
-        far = {(t, c): own[first + t, c] for t, c in index}
-    offsets = [near_first, 0]
-    cells = []
-    for t, c in index:
-        sides = [ref[offset + first + t, c].T for ref, offset in zip(beside, offsets)]
-        cells.append(jnp.concatenate([far[t, c], near[near_first + first + t, c]] + sides, axis=1))
-    filtered = jnp.dot(jnp.concatenate(cells, axis=0), walls[...], preferred_element_type=jnp.float32)
     keep = decay[...]
     fresh = jnp.sqrt(1.0 - keep * keep)
     line = lambda x, c: x[c : c + 1, :]
     u, d, o = mean[...], diag[...], off[...]
-    now = [state[c] for c in range(parts)]
-    for t in range(per):
+    band = walls[...]
+    now = [before[c] for c in range(parts)]
+    for first in range(0, count, 2):
+        group = range(first, min(first + 2, count))
+        if raw:
+            far = smooth_planes(1, start, first, len(group), weights, own, core, link)
+        for t in group:
+            step = start + t
+            q = max(q for q, at in enumerate(sources) if at <= step)
+            cells = []
+            for c in range(parts):
+                row = [far[t - first, c] if raw else own[t, c], near[q][step - sources[q], c]]
+                row += [ref[step - sources[q], c].T for ref in near_halo[q : q + 1]]
+                row += [ref[t, c].T for ref in far_halo]
+                cells.append(jnp.concatenate(row, axis=1))
+            filtered = jnp.dot(jnp.concatenate(cells, axis=0), band, preferred_element_type=jnp.float32)
+            for c in range(parts):
+                now[c] = line(keep, c) * now[c] + line(fresh, c) * filtered[c * rows : (c + 1) * rows]
+                value = line(u, c) + line(d, c) * now[c]
+                for e in range(c):
+                    value = value + line(o, (c * (c - 1)) // 2 + e) * now[e]
+                out[t, c] = value
+                if last:
+                    k = bool(kept) + t * parts + c
+                    copies.append(pltpu.make_async_copy(out.at[t, c], velocity.at[step, c], sems.at[k]))
+                    copies[-1].start()
+    if not last:
         for c in range(parts):
-            p = t * parts + c
-            now[c] = line(keep, c) * now[c] + line(fresh, c) * filtered[p * rows : (p + 1) * rows]
-        velocity[t, 0] = line(u, 0) + line(d, 0) * now[0]
-        velocity[t, 1] = line(u, 1) + line(o, 0) * now[0] + line(d, 1) * now[1]
-        velocity[t, 2] = line(u, 2) + line(o, 1) * now[0] + line(o, 2) * now[1] + line(d, 2) * now[2]
-    for c in range(parts):
-        state[c] = now[c]
+            state[c] = now[c]
+    for copy in copies:
+        copy.wait()
 
 
 def shards(random_fields, previous, decay, mean_flow, lund_diag, lund_off):
@@ -242,32 +257,47 @@
         far = [smooth(s, n, 1, far_core, link) for (s, n), link in zip(far_chunks, far_link)]
         far_halo = [lax.ppermute(edge, "gz", far_pairs) for _, edge in far]
 
-    velocity, state = None, previous
+    hbm = pl.BlockSpec(memory_space=pl.ANY)
+    velocity, state, kept = None, previous, None
     for k, (s, n) in enumerate(far_chunks):
-        source = max(q for q, (first, _) in enumerate(near_chunks) if first <= s)
-        per = math.gcd(math.gcd(n, s), 2)
+        last = k == len(far_chunks) - 1
+        used = [q for q, (at, count) in enumerate(near_chunks) if at < s + n and s < at + count]
         operands = [weights, walls, decay, mean_flow, lund_diag, lund_off, state]
-        operands += [own if far is None else far[k][0], far_core, far_link[k], near[source][0]]
-        beside = near_halo[source : source + 1] + far_halo[k : k + 1]
-        operands += beside
+        operands += [own if far is None else far[k][0], far_core, far_link[k]]
+        operands += [near[q][0] for q in used] + ([near_halo[q] for q in used] if near_halo else []) + far_halo[k : k + 1]
+        operands += [out] if k else []
         specs = [VMEM] * len(operands)
         aliases = {}
         if velocity is not None:
             aliases = {len(operands): 0}
             operands.append(velocity)
-            specs.append(pl.BlockSpec(memory_space=pl.ANY))
-        velocity, state = pl.pallas_call(
-            functools.partial(velocity_kernel, len(beside), far is None, s, s - near_chunks[source][0], per),
-            out_shape=(
-                jax.ShapeDtypeStruct((steps, parts, rows, cols), jnp.float32),
-                jax.ShapeDtypeStruct(previous.shape, jnp.float32),
+            specs.append(hbm)
+        held = jax.ShapeDtypeStruct((n, parts, rows, cols), jnp.float32)
+        shapes, places, scratch = [], [], []
+        if kept or last:
+            shapes.append(jax.ShapeDtypeStruct((steps, parts, rows, cols), jnp.float32))
+            places.append(hbm)
+        if last:
+            scratch.append(pltpu.VMEM(held.shape, held.dtype))
+        else:
+            shapes += [jax.ShapeDtypeStruct(previous.shape, jnp.float32), held]
+            places += [VMEM, VMEM]
+        if kept or last:
+            scratch.append(pltpu.SemaphoreType.DMA((bool(kept) + last * n * parts,)))
+        made = pl.pallas_call(
+            functools.partial(
+                velocity_kernel,
+                (s, n),
+                [near_chunks[q][0] for q in used],
+                far is None,
+                (bool(near_halo), bool(far_halo)),
+                kept,
+                last,
             ),
-            grid=(n // per,),
+            out_shape=shapes,
             in_specs=specs,
-            out_specs=(
-                pl.BlockSpec((per, parts, rows, cols), functools.partial(lambda o, t: (o + t, 0, 0, 0), s // per)),
-                VMEM,
-            ),
+            out_specs=places,
+            scratch_shapes=scratch,
             input_output_aliases=aliases,
             compiler_params=params,
             cost_estimate=pl.CostEstimate(
@@ -277,6 +307,10 @@
             ),
             name="velocity",
         )(*operands)
+        velocity = made[0] if kept or last else None
+        if not last:
+            state, out = made[-2:]
+        kept = (s, n)
     return velocity
 
 

time: 70.3 us -> 68.2 us (0.970)
  starting transfers between devices: 17 us -> 14.6 us
  waiting for transfers between devices: 37.4 us -> 39.5 us
  Pallas kernels: 12.7 us -> 10.8 us
    ppermute x7 -> x8, waiting for transfers between devices: 32.7 us -> 38.1 us  [shards(): lax.ppermute(x, 'gy', link_pairs)]
    ppermute x3 -> x4, waiting for transfers between devices: 4.76 us -> 1.39 us  [shards(): near_halo = [lax.ppermute(edge, 'gz', near_pairs) for _, edge in near]]
    pallas_call x4, Pallas kernels: 9.31 us -> 7.12 us  [shards(): pl.pallas_call(functools.partial(velocity_kernel, (s, n), [near_chunks[q]...]
    ppermute x7 -> x8, starting transfers between devices: 12.4 us -> 10.9 us  [shards(): lax.ppermute(x, 'gy', link_pairs)]
    ppermute x3 -> x4, starting transfers between devices: 4.01 us -> 3.12 us  [shards(): near_halo = [lax.ppermute(edge, 'gz', near_pairs) for _, edge in near]]
    pallas_call x3 -> x4, Pallas kernels: 2.28 us -> 2.52 us  [smooth(): pl.pallas_call(functools.partial(smooth_kernel, start, block, 3), out_sha...]
  transfers between devices with their start and end apart: 12 -> 14, of which waited for: 5 -> 4; matrix products, arithmetic and copies ran while one was open for 0% -> 0% of each run, Pallas kernels for 15% -> 13%
where the time goes in v2:
time: 68.2 us; the launch traced here: 68 us
  waiting for transfers between devices  39.5 us (58%)
  starting transfers between devices  14.6 us (21%)
  Pallas kernels  10.8 us (16%)
  local copies, waits for them, and re-layouts  2.87 us (4%)
    ppermute x8, waiting for transfers between devices, shards(): lax.ppermute(x, 'gy', link_pairs)  38.1 us
    ppermute x8, starting transfers between devices, shards(): lax.ppermute(x, 'gy', link_pairs)  10.9 us
    pallas_call x4, Pallas kernels, shards(): pl.pallas_call(functools.partial(velocity_kernel, (s, n), [near_chunks[q]...  7.12 us
    ppermute x4, starting transfers between devices, shards(): near_halo = [lax.ppermute(edge, 'gz', near_pairs) for _, edge in near]  3.12 us
    pallas_call x4, Pallas kernels, smooth(): pl.pallas_call(functools.partial(smooth_kernel, start, block, 3), out_sha...  2.52 us
    unnamed x14, local copies, waits for them, and re-layouts  1.92 us
    ppermute x4, waiting for transfers between devices, shards(): near_halo = [lax.ppermute(edge, 'gz', near_pairs) for _, edge in near]  1.39 us
  transfers between devices with their start and end apart: 14, of which 4 were waited for; matrix products, arithmetic and copies ran while one was open for 0% of the time, Pallas kernels for 13%

profile of v2, /device:TPU:1, one launch (start us, length us, event | category | flops | bytes accessed | tf_op | source)
XLA Modules:
  0.0 68.0 jit_solution(4502291964148762064)
XLA Ops:
  0.0 1.0 %constant_dynamic-slice_fusion = bf16[3,3,96,128]{3,2,1,0:T(8,128)(2,1)S(1)} fusion(bf16[16,3,128,256]{3,2,1,0:T(8,128)(2,1)} %refs_7_.3, s32[]{:T(128)S(6)} %select_n.18, s32[]{:T(128)S(6)} %select_n.20), kind=kLoop, calls=%fused_computation | loop fusion | bytes 442376 | tf_op jit(solution)/shard_map/dynamic_slice | solution.py:200
  1.0 0.0 copy-start
  1.0 1.9 %copy-done = bf16[16,3,128,256]{3,2,1,0:T(8,128)(2,1)S(1)} copy-done((bf16[16,3,128,256]{3,2,1,0:T(8,128)(2,1)S(1)}, bf16[16,3,128,256]{3,2,1,0:T(8,128)(2,1)}, u32[]{:S(2)}) %copy-start) | copy-done | bytes 3145752
  2.8 0.0 copy-start.1
  2.9 0.8 %pack.1 = (bf16[16,3,96,128]{3,2,1,0:T(8,128)(2,1)S(1)}, bf16[5,3,96,128]{3,2,1,0:T(8,128)(2,1)S(1)}, bf16[4,3,96,128]{3,2,1,0:T(8,128)(2,1)S(1)}, bf16[4,3,96,1...) custom-call(bf16[16,3,128,256]{3,2,1,0:T(8,128)(2,1)S(1)} %copy-done), custom_call_target="tpu_custom_call" | custom-call | tf_op jit(solution)/shard_map/pack/pallas_call | solution.py:209
  3.6 0.1 collective-permute-start.2
  3.7 0.5 collective-permute-start
  4.2 2.6 %collective-permute-start.4 = (bf16[5,3,96,128]{3,2,1,0:T(8,128)(2,1)S(1)}, bf16[5,3,96,128]{3,2,1,0:T(8,128)(2,1)S(1)}, u32[]{:S(2)}, u32[]{:S(2)}) collective-permute-start(bf16[5,3,96,128]{3,2,1,0:T(8,128)(2,1)S(1)} %get-tuple-element.42), channel_id=1, source_target_pairs={{2,4},{4,2},{6,8},{8,6},{10,12},{12,10},{14,16},{16,14},{18,20},{2... | collective-permute-start | bytes 1105928 | tf_op jit(solution)/shard_map/ppermute | solution.py:219
  6.8 0.0 collective-permute-start.1
  6.8 1.7 %collective-permute-start.8 = (bf16[4,3,96,128]{3,2,1,0:T(8,128)(2,1)S(1)}, bf16[4,3,96,128]{3,2,1,0:T(8,128)(2,1)S(1)}, u32[]{:S(2)}, u32[]{:S(2)}) collective-permute-start(bf16[4,3,96,128]{3,2,1,0:T(8,128)(2,1)S(1)} %get-tuple-element.48), channel_id=1, source_target_pairs={{2,4},{4,2},{6,8},{8,6},{10,12},{12,10},{14,16},{16,14},{18,20},{2... | collective-permute-start | bytes 884744 | tf_op jit(solution)/shard_map/ppermute | solution.py:219
  8.6 22.7 %collective-permute-done.4.link = bf16[5,3,96,128]{3,2,1,0:T(8,128)(2,1)S(1)} collective-permute-done((bf16[5,3,96,128]{3,2,1,0:T(8,128)(2,1)S(1)}, bf16[5,3,96,128]{3,2,1,0:T(8,128)(2,1)S(1)}, u32[]{:S(2)}, u32[]{:S(2)}) %collective-permute-start.4) | collective-permute-done | bytes 368672 | tf_op jit(solution)/shard_map/ppermute | solution.py:219
  31.3 1.4 %collective-permute-start.3 = (bf16[3,3,96,128]{3,2,1,0:T(8,128)(2,1)S(1)}, bf16[3,3,96,128]{3,2,1,0:T(8,128)(2,1)S(1)}, u32[]{:S(2)}, u32[]{:S(2)}) collective-permute-start(bf16[3,3,96,128]{3,2,1,0:T(8,128)(2,1)S(1)} %constant_dynamic-slice_fusion), channel_id=1, source_target_pairs={{2,4},{4,2},{6,8},{8,6},{10,12},{12,10},{14,16},{16,14},{18,20},{2... | collective-permute-start | bytes 663560 | tf_op jit(solution)/shard_map/ppermute | solution.py:219
  32.7 0.0 collective-permute-done.2.core
  32.7 0.3 collective-permute-start.11
  33.0 0.4 bands.1
  33.4 0.0 copy-done.1
  33.4 0.8 %smooth.5 = (bf16[5,3,128,128]{3,2,1,0:T(8,128)(2,1)S(1)}, bf16[5,3,96,128]{3,2,1,0:T(8,128)(2,1)S(1)}) custom-call(bf16[128,320]{1,0:T(8,128)(2,1)S(1)} %get-tuple-element.34.weights.refs_0_, bf16[16,3,128,256]{3,2,1,0:T(8,128)(2,1)S(1)} %copy-done.1, bf16[16,3,96,128]{3,2,1,0:T(8,128)(2,1)S(1)} %collective-permute-done.2.core, ...), custom_call_target="tpu_custom_call" | custom-call | flops 157286400 | bytes 1720320 | tf_op jit(solution)/shard_map/smooth/pallas_call | solution.py:235
  34.2 15.0 %collective-permute-done.3.link = bf16[3,3,96,128]{3,2,1,0:T(8,128)(2,1)S(1)} collective-permute-done((bf16[3,3,96,128]{3,2,1,0:T(8,128)(2,1)S(1)}, bf16[3,3,96,128]{3,2,1,0:T(8,128)(2,1)S(1)}, u32[]{:S(2)}, u32[]{:S(2)}) %collective-permute-start.3) | collective-permute-done | bytes 221216 | tf_op jit(solution)/shard_map/ppermute | solution.py:219
  49.1 1.4 %collective-permute-start.6 = (bf16[5,3,96,128]{3,2,1,0:T(8,128)(2,1)S(1)}, bf16[5,3,96,128]{3,2,1,0:T(8,128)(2,1)S(1)}, u32[]{:S(2)}, u32[]{:S(2)}) collective-permute-start(bf16[5,3,96,128]{3,2,1,0:T(8,128)(2,1)S(1)} %get-tuple-element.45), channel_id=1, source_target_pairs={{0,1},{1,0},{2,3},{3,2},{4,5},{5,4},{6,7},{7,6},{8,9},{9,8},{10,11... | collective-permute-start | bytes 1105928 | tf_op jit(solution)/shard_map/ppermute | solution.py:255
  50.5 0.4 smooth.4
  50.9 0.0 collective-permute-done.8.link
  50.9 0.2 collective-permute-start.5
  51.1 0.7 %smooth.6 = (bf16[4,3,128,128]{3,2,1,0:T(8,128)(2,1)S(1)}, bf16[4,3,96,128]{3,2,1,0:T(8,128)(2,1)S(1)}) custom-call(bf16[128,320]{1,0:T(8,128)(2,1)S(1)} %get-tuple-element.34.weights.refs_0_, bf16[16,3,128,256]{3,2,1,0:T(8,128)(2,1)S(1)} %copy-done.1, bf16[16,3,96,128]{3,2,1,0:T(8,128)(2,1)S(1)} %collective-permute-done.2.core, ...), custom_call_target="tpu_custom_call" | custom-call | flops 125829120 | bytes 1376256 | tf_op jit(solution)/shard_map/smooth/pallas_call | solution.py:235
  51.8 0.0 copy-start.2
  51.8 0.0 copy-start.3
  51.8 0.0 copy-start.4
  51.8 0.0 copy-start.5
  51.8 0.0 copy-start.6
  51.8 0.5 collective-permute-done.11.link
  52.3 1.9 %collective-permute-start.7 = (bf16[4,3,96,128]{3,2,1,0:T(8,128)(2,1)S(1)}, bf16[4,3,96,128]{3,2,1,0:T(8,128)(2,1)S(1)}, u32[]{:S(2)}, u32[]{:S(2)}) collective-permute-start(bf16[4,3,96,128]{3,2,1,0:T(8,128)(2,1)S(1)} %get-tuple-element.47), channel_id=1, source_target_pairs={{2,4},{4,2},{6,8},{8,6},{10,12},{12,10},{14,16},{16,14},{18,20},{2... | collective-permute-start | bytes 884744 | tf_op jit(solution)/shard_map/ppermute | solution.py:219
  54.2 0.0 collective-permute-done.1.refs_9_
  54.2 1.2 %collective-permute-start.9 = (bf16[4,3,96,128]{3,2,1,0:T(8,128)(2,1)S(1)}, bf16[4,3,96,128]{3,2,1,0:T(8,128)(2,1)S(1)}, u32[]{:S(2)}, u32[]{:S(2)}) collective-permute-start(bf16[4,3,96,128]{3,2,1,0:T(8,128)(2,1)S(1)} %get-tuple-element.50), channel_id=1, source_target_pairs={{0,1},{1,0},{2,3},{3,2},{4,5},{5,4},{6,7},{7,6},{8,9},{9,8},{10,11... | collective-permute-start | bytes 884744 | tf_op jit(solution)/shard_map/ppermute | solution.py:255
  55.5 0.7 %smooth.7 = (bf16[4,3,128,128]{3,2,1,0:T(8,128)(2,1)S(1)}, bf16[4,3,96,128]{3,2,1,0:T(8,128)(2,1)S(1)}) custom-call(bf16[128,320]{1,0:T(8,128)(2,1)S(1)} %get-tuple-element.34.weights.refs_0_, bf16[16,3,128,256]{3,2,1,0:T(8,128)(2,1)S(1)} %copy-done.1, bf16[16,3,96,128]{3,2,1,0:T(8,128)(2,1)S(1)} %collective-permute-done.2.core, ...), custom_call_target="tpu_custom_call" | custom-call | flops 125829120 | bytes 1376256 | tf_op jit(solution)/shard_map/smooth/pallas_call | solution.py:235
  56.1 0.0 collective-permute-done.refs_8_
  56.2 0.3 collective-permute-start.12
  56.5 1.4 %collective-permute-done.5.refs_12_ = bf16[3,3,96,128]{3,2,1,0:T(8,128)(2,1)S(1)} collective-permute-done((bf16[3,3,96,128]{3,2,1,0:T(8,128)(2,1)S(1)}, bf16[3,3,96,128]{3,2,1,0:T(8,128)(2,1)S(1)}, u32[]{:S(2)}, u32[]{:S(2)}) %collective-permute-start.5) | collective-permute-done | bytes 221216 | tf_op jit(solution)/shard_map/ppermute | solution.py:255
  57.9 2.9 %collective-permute-start.10 = (bf16[3,3,96,128]{3,2,1,0:T(8,128)(2,1)S(1)}, bf16[3,3,96,128]{3,2,1,0:T(8,128)(2,1)S(1)}, u32[]{:S(2)}, u32[]{:S(2)}) collective-permute-start(bf16[3,3,96,128]{3,2,1,0:T(8,128)(2,1)S(1)} %get-tuple-element.53), channel_id=1, source_target_pairs={{2,4},{4,2},{6,8},{8,6},{10,12},{12,10},{14,16},{16,14},{18,20},{2... | collective-permute-start | bytes 663560 | tf_op jit(solution)/shard_map/ppermute | solution.py:219
  60.8 0.0 collective-permute-done.6.refs_13_
  60.8 0.0 collective-permute-start.13
  60.8 0.0 copy-done.2
  60.8 0.0 copy-done.3
  60.8 0.0 copy-done.4
  60.8 0.0 copy-done.5
  60.8 0.0 copy-done.6
  60.8 2.0 %velocity.4 = (f32[3,128,256]{2,1,0:T(8,128)S(1)}, f32[8,3,128,256]{3,2,1,0:T(8,128)S(1)}) custom-call(bf16[128,320]{1,0:T(8,128)(2,1)S(1)} %get-tuple-element.34.weights.refs_0_, bf16[352,256]{1,0:T(8,128)(2,1)S(1)} %get-tuple-element.35.refs_1_, f32[3,256]{1,0:T(4,128)S(1)} %copy-done.3, f32[3,256]{1,0:T(4,128)S(1)} %copy-done.4, f32[3,256]{1,0:T(4,128)S(1)} %copy-done.5, ...), custom_call_target="tpu_custom_call" | custom-call | flops 805306368 | bytes 7077888 | tf_op jit(solution)/shard_map/velocity/pallas_call | solution.py:287
  62.8 0.0 collective-permute-done.7.refs_9_
  62.8 0.0 collective-permute-done.9.refs_11_
  62.8 2.2 %velocity.5 = (f32[16,3,128,256]{3,2,1,0:T(8,128)}, f32[3,128,256]{2,1,0:T(8,128)S(1)}, f32[4,3,128,256]{3,2,1,0:T(8,128)S(1)}) custom-call(bf16[128,320]{1,0:T(8,128)(2,1)S(1)} %get-tuple-element.34.weights.refs_0_, bf16[352,256]{1,0:T(8,128)(2,1)S(1)} %get-tuple-element.35.refs_1_, f32[3,256]{1,0:T(4,128)S(1)} %copy-done.3, f32[3,256]{1,0:T(4,128)S(1)} %copy-done.4, ...), custom_call_target="tpu_custom_call" | custom-call | flops 402653184 | bytes 3538944 | tf_op jit(solution)/shard_map/velocity/pallas_call | solution.py:287
  65.0 0.0 collective-permute-done.10.refs_9_
  65.0 0.0 collective-permute-done.12.refs_11_
  65.0 1.8 %velocity.6 = (f32[16,3,128,256]{3,2,1,0:T(8,128)}, f32[3,128,256]{2,1,0:T(8,128)S(1)}, f32[3,3,128,256]{3,2,1,0:T(8,128)S(1)}) custom-call(bf16[128,320]{1,0:T(8,128)(2,1)S(1)} %get-tuple-element.34.weights.refs_0_, bf16[352,256]{1,0:T(8,128)(2,1)S(1)} %get-tuple-element.35.refs_1_, f32[3,256]{1,0:T(4,128)S(1)} %copy-done.3, ...), custom_call_target="tpu_custom_call", output_to_operand_aliasing={{0}: (13, {})} | custom-call | flops 301989888 | bytes 2654208 | tf_op jit(solution)/shard_map/velocity/pallas_call | solution.py:287
  66.8 0.0 collective-permute-done.13.refs_9_
  66.8 1.2 %velocity.7 = f32[16,3,128,256]{3,2,1,0:T(8,128)} custom-call(bf16[128,320]{1,0:T(8,128)(2,1)S(1)} %get-tuple-element.34.weights.refs_0_, bf16[352,256]{1,0:T(8,128)(2,1)S(1)} %get-tuple-element.35.refs_1_, f32[3,256]{1,0:T(4,128)S(1)} %copy-done.3, f32[3,256]{1,0:T(4,128)S(1)} %copy-done.4, ...), custom_call_target="tpu_custom_call", output_to_operand_aliasing={{}: (13, {})} | custom-call | flops 100663296 | bytes 884736 | tf_op jit(solution)/shard_map/velocity/pallas_call | solution.py:287
Async XLA Ops:
  1.0 1.9 %copy-start = (bf16[16,3,128,256]{3,2,1,0:T(8,128)(2,1)S(1)}, bf16[16,3,128,256]{3,2,1,0:T(8,128)(2,1)}, u32[]{:S(2)}) copy-start(bf16[16,3,128,256]{3,2,1,0:T(8,128)(2,1)} %refs_7_.3) | copy-start | bytes 9437188
  2.8 30.5 %copy-start.1 = (bf16[16,3,128,256]{3,2,1,0:T(8,128)(2,1)S(1)}, bf16[16,3,128,256]{3,2,1,0:T(8,128)(2,1)}, u32[]{:S(2)}) copy-start(bf16[16,3,128,256]{3,2,1,0:T(8,128)(2,1)} %refs_7_.3) | copy-start | bytes 9437188
  3.6 29.1 %collective-permute-start.2 = (bf16[16,3,96,128]{3,2,1,0:T(8,128)(2,1)S(1)}, bf16[16,3,96,128]{3,2,1,0:T(8,128)(2,1)S(1)}, u32[]{:S(2)}, u32[]{:S(2)}) collective-permute-start(bf16[16,3,96,128]{3,2,1,0:T(8,128)(2,1)S(1)} %get-tuple-element.39), channel_id=1, source_target_pairs={{0,2},{2,0},{4,6},{6,4},{8,10},{10,8},{12,14},{14,12},{16,18},{18,... | collective-permute-start | bytes 3538952 | tf_op jit(solution)/shard_map/ppermute | solution.py:217
  3.7 52.4 %collective-permute-start = (bf16[16,3,96,128]{3,2,1,0:T(8,128)(2,1)S(1)}, bf16[16,3,96,128]{3,2,1,0:T(8,128)(2,1)S(1)}, u32[]{:S(2)}, u32[]{:S(2)}) collective-permute-start(bf16[16,3,96,128]{3,2,1,0:T(8,128)(2,1)S(1)} %get-tuple-element.37), channel_id=1, source_target_pairs={{0,2},{2,0},{4,6},{6,4},{8,10},{10,8},{12,14},{14,12},{16,18},{18,... | collective-permute-start | bytes 3538952 | tf_op jit(solution)/shard_map/ppermute | solution.py:218
  4.2 27.1 %collective-permute-start.4 = (bf16[5,3,96,128]{3,2,1,0:T(8,128)(2,1)S(1)}, bf16[5,3,96,128]{3,2,1,0:T(8,128)(2,1)S(1)}, u32[]{:S(2)}, u32[]{:S(2)}) collective-permute-start(bf16[5,3,96,128]{3,2,1,0:T(8,128)(2,1)S(1)} %get-tuple-element.42), channel_id=1, source_target_pairs={{2,4},{4,2},{6,8},{8,6},{10,12},{12,10},{14,16},{16,14},{18,20},{2... | collective-permute-start | bytes 1105928 | tf_op jit(solution)/shard_map/ppermute | solution.py:219
  6.8 47.4 %collective-permute-start.1 = (bf16[8,3,96,128]{3,2,1,0:T(8,128)(2,1)S(1)}, bf16[8,3,96,128]{3,2,1,0:T(8,128)(2,1)S(1)}, u32[]{:S(2)}, u32[]{:S(2)}) collective-permute-start(bf16[8,3,96,128]{3,2,1,0:T(8,128)(2,1)S(1)} %get-tuple-element.38), channel_id=1, source_target_pairs={{2,4},{4,2},{6,8},{8,6},{10,12},{12,10},{14,16},{16,14},{18,20},{2... | collective-permute-start | bytes 1769480 | tf_op jit(solution)/shard_map/ppermute | solution.py:219
  6.8 44.1 %collective-permute-start.8 = (bf16[4,3,96,128]{3,2,1,0:T(8,128)(2,1)S(1)}, bf16[4,3,96,128]{3,2,1,0:T(8,128)(2,1)S(1)}, u32[]{:S(2)}, u32[]{:S(2)}) collective-permute-start(bf16[4,3,96,128]{3,2,1,0:T(8,128)(2,1)S(1)} %get-tuple-element.48), channel_id=1, source_target_pairs={{2,4},{4,2},{6,8},{8,6},{10,12},{12,10},{14,16},{16,14},{18,20},{2... | collective-permute-start | bytes 884744 | tf_op jit(solution)/shard_map/ppermute | solution.py:219
  31.3 17.9 %collective-permute-start.3 = (bf16[3,3,96,128]{3,2,1,0:T(8,128)(2,1)S(1)}, bf16[3,3,96,128]{3,2,1,0:T(8,128)(2,1)S(1)}, u32[]{:S(2)}, u32[]{:S(2)}) collective-permute-start(bf16[3,3,96,128]{3,2,1,0:T(8,128)(2,1)S(1)} %constant_dynamic-slice_fusion), channel_id=1, source_target_pairs={{2,4},{4,2},{6,8},{8,6},{10,12},{12,10},{14,16},{16,14},{18,20},{2... | collective-permute-start | bytes 663560 | tf_op jit(solution)/shard_map/ppermute | solution.py:219
  32.7 19.6 %collective-permute-start.11 = (bf16[4,3,96,128]{3,2,1,0:T(8,128)(2,1)S(1)}, bf16[4,3,96,128]{3,2,1,0:T(8,128)(2,1)S(1)}, u32[]{:S(2)}, u32[]{:S(2)}) collective-permute-start(bf16[4,3,96,128]{3,2,1,0:T(8,128)(2,1)S(1)} %get-tuple-element.54), channel_id=1, source_target_pairs={{2,4},{4,2},{6,8},{8,6},{10,12},{12,10},{14,16},{16,14},{18,20},{2... | collective-permute-start | bytes 884744 | tf_op jit(solution)/shard_map/ppermute | solution.py:219
  49.1 11.6 %collective-permute-start.6 = (bf16[5,3,96,128]{3,2,1,0:T(8,128)(2,1)S(1)}, bf16[5,3,96,128]{3,2,1,0:T(8,128)(2,1)S(1)}, u32[]{:S(2)}, u32[]{:S(2)}) collective-permute-start(bf16[5,3,96,128]{3,2,1,0:T(8,128)(2,1)S(1)} %get-tuple-element.45), channel_id=1, source_target_pairs={{0,1},{1,0},{2,3},{3,2},{4,5},{5,4},{6,7},{7,6},{8,9},{9,8},{10,11... | collective-permute-start | bytes 1105928 | tf_op jit(solution)/shard_map/ppermute | solution.py:255
  50.9 6.9 %collective-permute-start.5 = (bf16[3,3,96,128]{3,2,1,0:T(8,128)(2,1)S(1)}, bf16[3,3,96,128]{3,2,1,0:T(8,128)(2,1)S(1)}, u32[]{:S(2)}, u32[]{:S(2)}) collective-permute-start(bf16[3,3,96,128]{3,2,1,0:T(8,128)(2,1)S(1)} %get-tuple-element.44), channel_id=1, source_target_pairs={{0,1},{1,0},{2,3},{3,2},{4,5},{5,4},{6,7},{7,6},{8,9},{9,8},{10,11... | collective-permute-start | bytes 663560 | tf_op jit(solution)/shard_map/ppermute | solution.py:255
  51.8 9.0 %copy-start.2 = (f32[3,128,256]{2,1,0:T(8,128)S(1)}, f32[3,128,256]{2,1,0:T(8,128)}, u32[]{:S(2)}) copy-start(f32[3,128,256]{2,1,0:T(8,128)} %refs_6_.1) | copy-start | bytes 1179652
  51.8 9.0 %copy-start.3 = (f32[3,256]{1,0:T(4,128)S(1)}, f32[3,256]{1,0:T(4,128)}, u32[]{:S(2)}) copy-start(f32[3,256]{1,0:T(4,128)} %refs_2_.7) | copy-start | bytes 9220
  51.8 9.0 %copy-start.4 = (f32[3,256]{1,0:T(4,128)S(1)}, f32[3,256]{1,0:T(4,128)}, u32[]{:S(2)}) copy-start(f32[3,256]{1,0:T(4,128)} %refs_3_.7) | copy-start | bytes 9220
  51.8 9.0 %copy-start.5 = (f32[3,256]{1,0:T(4,128)S(1)}, f32[3,256]{1,0:T(4,128)}, u32[]{:S(2)}) copy-start(f32[3,256]{1,0:T(4,128)} %refs_4_.7) | copy-start | bytes 9220
  51.8 9.0 %copy-start.6 = (f32[3,256]{1,0:T(4,128)S(1)}, f32[3,256]{1,0:T(4,128)}, u32[]{:S(2)}) copy-start(f32[3,256]{1,0:T(4,128)} %refs_5_.7) | copy-start | bytes 9220
  52.3 10.5 %collective-permute-start.7 = (bf16[4,3,96,128]{3,2,1,0:T(8,128)(2,1)S(1)}, bf16[4,3,96,128]{3,2,1,0:T(8,128)(2,1)S(1)}, u32[]{:S(2)}, u32[]{:S(2)}) collective-permute-start(bf16[4,3,96,128]{3,2,1,0:T(8,128)(2,1)S(1)} %get-tuple-element.47), channel_id=1, source_target_pairs={{2,4},{4,2},{6,8},{8,6},{10,12},{12,10},{14,16},{16,14},{18,20},{2... | collective-permute-start | bytes 884744 | tf_op jit(solution)/shard_map/ppermute | solution.py:219
  54.2 8.6 %collective-permute-start.9 = (bf16[4,3,96,128]{3,2,1,0:T(8,128)(2,1)S(1)}, bf16[4,3,96,128]{3,2,1,0:T(8,128)(2,1)S(1)}, u32[]{:S(2)}, u32[]{:S(2)}) collective-permute-start(bf16[4,3,96,128]{3,2,1,0:T(8,128)(2,1)S(1)} %get-tuple-element.50), channel_id=1, source_target_pairs={{0,1},{1,0},{2,3},{3,2},{4,5},{5,4},{6,7},{7,6},{8,9},{9,8},{10,11... | collective-permute-start | bytes 884744 | tf_op jit(solution)/shard_map/ppermute | solution.py:255
  56.2 8.8 %collective-permute-start.12 = (bf16[4,3,96,128]{3,2,1,0:T(8,128)(2,1)S(1)}, bf16[4,3,96,128]{3,2,1,0:T(8,128)(2,1)S(1)}, u32[]{:S(2)}, u32[]{:S(2)}) collective-permute-start(bf16[4,3,96,128]{3,2,1,0:T(8,128)(2,1)S(1)} %get-tuple-element.56), channel_id=1, source_target_pairs={{0,1},{1,0},{2,3},{3,2},{4,5},{5,4},{6,7},{7,6},{8,9},{9,8},{10,11... | collective-permute-start | bytes 884744 | tf_op jit(solution)/shard_map/ppermute | solution.py:255
  57.9 7.1 %collective-permute-start.10 = (bf16[3,3,96,128]{3,2,1,0:T(8,128)(2,1)S(1)}, bf16[3,3,96,128]{3,2,1,0:T(8,128)(2,1)S(1)}, u32[]{:S(2)}, u32[]{:S(2)}) collective-permute-start(bf16[3,3,96,128]{3,2,1,0:T(8,128)(2,1)S(1)} %get-tuple-element.53), channel_id=1, source_target_pairs={{2,4},{4,2},{6,8},{8,6},{10,12},{12,10},{14,16},{16,14},{18,20},{2... | collective-permute-start | bytes 663560 | tf_op jit(solution)/shard_map/ppermute | solution.py:219
  60.8 6.1 %collective-permute-start.13 = (bf16[1,3,96,128]{3,2,1,0:T(8,128)(2,1)S(1)}, bf16[1,3,96,128]{3,2,1,0:T(8,128)(2,1)S(1)}, u32[]{:S(2)}, u32[]{:S(2)}) collective-permute-start(bf16[1,3,96,128]{3,2,1,0:T(8,128)(2,1)S(1)} %get-tuple-element.60), channel_id=1, source_target_pairs={{2,4},{4,2},{6,8},{8,6},{10,12},{12,10},{14,16},{16,14},{18,20},{2... | collective-permute-start | bytes 221192 | tf_op jit(solution)/shard_map/ppermute | solution.py:219
